TPU v7x, 128 devices: a whole 4x4x4 slice. The times are simulated.
128 devices in a mesh: dp: 8 (over x, core), tensor: 16 (over z, y).
Axes of the slice: x: 4, y: 4, z: 4, core: 2. Of those that a mesh axis runs over, the one named last changes fastest.
Arguments:
- attn_ctx: bfloat16 [4096, 8192], P('dp', 'tensor'), may hold values from -6 to 6
- w_out: bfloat16 [8192, 8192], P('tensor'), may hold values from -0.09375 to 0.09375
- resid: bfloat16 [4096, 8192], P(('dp', 'tensor')), may hold values from -6 to 6
- teacher_gain: bfloat16 [8192], replicated, may hold values from 0.25 to 1.75
- dest_row: int32 [4096], replicated, may hold values from 0 to 4095, as said below
- student_in: bfloat16 [4096, 4096], P('dp', 'tensor'), may hold values from -6 to 6
- student_gain: bfloat16 [4096], replicated, may hold values from 0.25 to 1.75
- w_gate: bfloat16 [4096, 14336], P('dp', 'tensor'), may hold values from -0.09375 to 0.09375
- w_up: bfloat16 [4096, 14336], P('dp', 'tensor'), may hold values from -0.09375 to 0.09375
- w_down: bfloat16 [14336, 4096], P('tensor', 'dp'), may hold values from -0.0625 to 0.0625
- proj: bfloat16 [4096, 8192], P('dp', 'tensor'), may hold values from -0.09375 to 0.09375
Outputs:
- student_out: bfloat16 [4096, 4096], P('dp', 'tensor')
- row_loss: float32 [4096], P('dp')
- residue: float32 [4096, 8192], P('dp', 'tensor')
Inputs may be any that keep to these rules, and one draw needn't show every extreme that they name: A permutation of the rows; of the 32 rows i in one aligned block of teacher rows, at most 8 have dest_row[i] in any one tile of 512 student rows, and some tile receives exactly 8 of them.
All inputs are finite; a program needn't handle non-finite values.
Results may differ from a plain program's by a relative error of at most 0.012.
Values may be sent and summed in bfloat16 or wider, within the bound.
A program may use at most 128 MiB of HBM per device.

v0:
```python
import jax
import jax.numpy as jnp
from jax import lax
from jax.sharding import Mesh
from jax.sharding import PartitionSpec as P

HT = 8192
TENSOR = ("tensor_0", "tensor_1")
DP_TENSOR = ("dp", "tensor_0", "tensor_1")


def whole_of(value, axes, dim):
    if not axes:
        return value
    nearer = lax.all_gather(value, axes[-1], axis=dim, tiled=True)
    return whole_of(nearer, axes[:-1], dim)


def in_one_piece(arrays, axis, dim, along):
    both = jnp.concatenate(arrays, axis=along)
    filled, at, done = (lax.all_gather(both, axis, axis=dim, tiled=True), 0, [])
    for a in arrays:
        done.append(lax.slice_in_dim(filled, at, at + a.shape[along], axis=along))
        at += a.shape[along]
    return tuple(done)


def one_axis_at_a_time(value, axes):
    for axis in axes:
        value = lax.psum(value, axis)
    return value


def local(
    attn_ctx,
    w_out,
    resid,
    teacher_gain,
    dest_row,
    student_in,
    student_gain,
    w_gate,
    w_up,
    w_down,
    proj,
):
    tensor_count = lax.axis_size(TENSOR)
    group_count = lax.axis_size("dp")
    tile_rows = attn_ctx.shape[0]
    own_rows = resid.shape[0]
    portion = attn_ctx
    summed = lax.psum_scatter(
        jnp.dot(portion, w_out, preferred_element_type=jnp.float32).astype(jnp.bfloat16),
        TENSOR,
        scatter_dimension=0,
        tiled=True,
    ).astype(jnp.float32)
    teacher_hidden = resid.astype(jnp.float32) + summed
    square_mean = jnp.mean(teacher_hidden * teacher_hidden, axis=1, keepdims=True)
    teacher_final = (
        teacher_hidden * lax.rsqrt(square_mean + 1e-06) * teacher_gain.astype(jnp.float32)
    ).astype(jnp.bfloat16)
    capacity = 2 * own_rows // group_count
    source_count = group_count * tensor_count
    group_ids = (dest_row // tile_rows).reshape(source_count, own_rows)
    onehot = (group_ids[:, :, None] == jnp.arange(group_count)[None, None, :]).astype(jnp.int32)
    slot_index = jnp.sum((jnp.cumsum(onehot, 1) - onehot) * onehot, 2)
    my_source = lax.axis_index("dp") * tensor_count + lax.axis_index(TENSOR)
    own_groups = lax.dynamic_index_in_dim(group_ids, my_source, 0, keepdims=False)
    own_slots = lax.dynamic_index_in_dim(slot_index, my_source, 0, keepdims=False)
    target_slot = own_groups * capacity + own_slots
    selector = (target_slot[None, :] == jnp.arange(group_count * capacity)[:, None]).astype(
        jnp.bfloat16
    )
    packed = jnp.dot(selector, teacher_final, preferred_element_type=jnp.float32).astype(
        jnp.bfloat16
    )
    col_width = teacher_final.shape[1] // tensor_count
    send_blocks = packed.reshape(group_count, capacity, tensor_count, col_width).transpose(
        0, 2, 1, 3
    )
    arrived = lax.all_to_all(
        send_blocks.reshape(source_count, capacity, col_width),
        DP_TENSOR,
        split_axis=0,
        concat_axis=0,
        tiled=True,
    )
    flattened = arrived.reshape(source_count * capacity, col_width)
    arrival_index = (jnp.arange(source_count)[:, None] * capacity + slot_index).reshape(-1)
    inverse = jnp.zeros(dest_row.shape, jnp.int32).at[dest_row].set(arrival_index)
    own_arrivals = lax.dynamic_slice_in_dim(inverse, lax.axis_index("dp") * tile_rows, tile_rows, 0)
    target = jnp.take(flattened, own_arrivals, axis=0)
    gathered = whole_of(student_in, TENSOR, 1)
    x_full = gathered.astype(jnp.float32)
    student_mean = jnp.mean(x_full * x_full, axis=1, keepdims=True)
    normed = (x_full * lax.rsqrt(student_mean + 1e-05) * student_gain.astype(jnp.float32)).astype(
        jnp.bfloat16
    )

    def add_rows(portion):
        return jnp.dot(normed, portion, preferred_element_type=jnp.float32)

    portions = in_one_piece((w_gate, w_up), "dp", 0, 1)
    gate_acts = add_rows(portions[0])
    up_acts = add_rows(portions[1])
    hidden = (jax.nn.silu(gate_acts) * up_acts).astype(jnp.bfloat16)
    partial_sum = jnp.dot(
        hidden, lax.all_gather(w_down, "dp", axis=1, tiled=True), preferred_element_type=jnp.float32
    )
    local_cols = student_in.shape[1]
    mlp_sum = lax.psum(partial_sum.astype(jnp.bfloat16), TENSOR).astype(jnp.float32)
    out_full = (x_full + mlp_sum).astype(jnp.bfloat16)
    out_local = lax.dynamic_slice_in_dim(
        out_full, lax.axis_index(TENSOR) * local_cols, local_cols, 1
    )
    pred = jnp.dot(
        out_full, lax.all_gather(proj, "dp", axis=0, tiled=True), preferred_element_type=jnp.float32
    )
    residue = pred - target.astype(jnp.float32)
    row_error = jnp.sum(residue * residue, axis=1)
    row_loss = one_axis_at_a_time(row_error, TENSOR) / HT
    return (out_local, row_loss, residue)


def solution(mesh):
    torus = Mesh(mesh.devices.reshape(mesh.shape["dp"], 4, 4), ("dp", "tensor_0", "tensor_1"))
    in_specs = (
        P("dp", TENSOR),
        P(TENSOR, None),
        P(DP_TENSOR, None),
        P(),
        P(),
        P("dp", TENSOR),
        P(),
        P("dp", TENSOR),
        P("dp", TENSOR),
        P(TENSOR, "dp"),
        P("dp", TENSOR),
    )
    out_specs = (P("dp", TENSOR), P("dp"), P("dp", TENSOR))
    return jax.shard_map(local, mesh=torus, in_specs=in_specs, out_specs=out_specs, check_vma=False)
```

profile of v0, /device:TPU:0, one launch (start us, length us, event | category | flops | bytes accessed | tf_op | source)
XLA Modules:
  0.0 386.2 jit_solution(12884927231621667564)
XLA Ops:
  8.0 0.0 copy-start
  8.0 0.0 all-gather.6.cloned.1.call-start
  8.1 0.7 all-gather.6.cloned.1.call-update
  8.7 0.0 all-gather.8.cloned.1.call-start
  8.8 29.6 %all-gather.6.cloned.1.call-done = bf16[512,1024]{1,0:T(8,128)(2,1)} async-done(((bf16[512,256]{1,0:T(8,128)(2,1)}), bf16[512,1024]{1,0:T(8,128)(2,1)}) %all-gather.6.cloned.1.call-update) | async-done | bytes 1048592 | tf_op jit(solution)/shard_map/all_gather | solution.py:15
  38.4 0.0 all-gather.8.cloned.1.call-update
  38.4 0.0 all-gather.10.cloned.1.call-start
  38.5 2.8 pad_maximum_fusion
  41.3 0.0 all-gather.10.cloned.1.call-update
  41.3 0.0 all-gather.12.cloned.1.call-start
  41.4 0.5 all-gather.12.cloned.1.call-update
  41.9 0.0 reduce-scatter.2.cloned.1.call-start
  42.0 0.0 copy-done
  42.0 10.1 %convolution_convert_fusion = bf16[512,8192]{1,0:T(8,128)(2,1)} fusion(bf16[512,512]{1,0:T(8,128)(2,1)S(1)} %copy-done, bf16[512,8192]{1,0:T(8,128)(2,1)} %param.12), kind=kOutput, calls=%fused_computation.5 | convolution fusion | flops 4299161600 | bytes 17301504 | tf_op jit(solution)/shard_map/dot_general | solution.py:53
  52.1 0.0 copy-start.7
  52.1 0.0 reduce-scatter.2.cloned.1.call-update
  52.1 0.2 all-reduce.2.cloned.1.call-start
  52.4 0.4 copy-done.7
  52.8 42.6 %all-gather.8.cloned.1.call-done = bf16[512,4096]{1,0:T(8,128)(2,1)} async-done(((bf16[512,1024]{1,0:T(8,128)(2,1)}), bf16[512,4096]{1,0:T(8,128)(2,1)}) %all-gather.8.cloned.1.call-update) | async-done | bytes 4194320 | tf_op jit(solution)/shard_map/all_gather | solution.py:15
  95.4 3.2 fusion
  98.6 74.7 %all-gather.10.cloned.1.call-done = bf16[4096,1792]{1,0:T(8,128)(2,1)} async-done(((bf16[512,1792]{1,0:T(8,128)(2,1)}), bf16[4096,1792]{1,0:T(8,128)(2,1)}) %all-gather.10.cloned.1.call-update) | async-done | bytes 14680080 | tf_op jit(solution)/shard_map/all_gather | solution.py:21
  173.4 0.0 copy-start.2
  173.4 0.0 copy-start.8
  173.4 11.3 %fusion.6 = f32[512,896]{1,0:T(8,128)S(1)} fusion(bf16[4096,1792]{1,0:T(8,128)(2,1)} %all-gather.10.cloned.1.call-done, bf16[512,4096]{1,0:T(8,128)(2,1)} %all-gather.8.cloned.1.call-done, f32[4096]{0:T(1024)S(1)} %convert_element_type.47, f32[512]{0:T(512)S(1)} %add_rsqrt_fusion), kind=kOutput, calls=%fused_computation.13 | convolution fusion | flops 3766484992 | bytes 13387776 | tf_op jit(solution)/shard_map/dot_general | solution.py:102
  184.6 0.0 copy-done.2
  184.6 0.0 copy-done.8
  184.6 4.6 %multiply_convert_fusion = bf16[512,896]{1,0:T(8,128)(2,1)S(1)} fusion(f32[512,896]{1,0:T(8,128)S(1)} %fusion.6, bf16[4096,1792]{1,0:T(8,128)(2,1)S(1)} %copy-done.8, bf16[512,4096]{1,0:T(8,128)(2,1)S(1)} %copy-done.2, f32[4096]{0:T(1024)S(1)} %convert_element_type.47, f32[512]{0:T(512)S(1)} %add_rsqrt_fusion), kind=kOutput, calls=%fused_computation.17 | convolution fusion | flops 3769237504 | bytes 14305280 | tf_op jit(solution)/shard_map/dot_general | solution.py:102
  189.3 31.4 %all-gather.12.cloned.1.call-done = bf16[896,4096]{1,0:T(8,128)(2,1)} async-done(((bf16[896,512]{1,0:T(8,128)(2,1)}), bf16[896,4096]{1,0:T(8,128)(2,1)}) %all-gather.12.cloned.1.call-update) | async-done | bytes 7340048 | tf_op jit(solution)/shard_map/all_gather | solution.py:109
  220.7 9.1 %convolution_convert_fusion.2 = bf16[512,4096]{1,0:T(8,128)(2,1)} fusion(bf16[512,896]{1,0:T(8,128)(2,1)S(1)} %multiply_convert_fusion, bf16[896,4096]{1,0:T(8,128)(2,1)} %all-gather.12.cloned.1.call-done), kind=kOutput, calls=%fused_computation.15 | convolution fusion | flops 3760193536 | bytes 12451840 | tf_op jit(solution)/shard_map/dot_general | solution.py:108
  229.8 0.0 copy-start.5
  229.8 0.0 copy-start.6
  229.8 0.0 copy-start.4
  229.8 0.0 all-reduce.2.cloned.1.call-update
  229.8 0.0 all-gather.14.cloned.1.call-start
  229.9 0.5 all-gather.14.cloned.1.call-update
  230.4 0.1 copy-done.5
  230.5 0.0 copy-done.6
  230.5 0.1 eq.30
  230.6 0.1 copy.25
  230.7 0.1 fusion.22
  230.7 0.2 add_reduce_fusion
  230.9 0.0 reduce-scatter.2.cloned.1.call-done
  231.0 0.0 copy-done.4
  231.0 1.3 multiply_reduce_fusion.1
  232.3 2.5 convolution_convert_fusion.1
  234.8 8.8 %all-to-all-start = ((bf16[128,8,512]{2,1,0:T(8,128)(2,1)}), bf16[128,8,512]{2,1,0:T(8,128)(2,1)S(1)}, u32[]{:S(2)}, u32[]{:S(2)}) async-start(bf16[128,8,512]{2,1,0:T(8,128)(2,1)} %bitcast.2), calls=%async_computation.1 | async-start | bytes 2097152 | tf_op jit(solution)/shard_map/all_to_all | solution.py:82
  243.7 0.1 copy.26
  243.8 0.1 reshape.64
  243.8 15.8 %scatter_custom_fusion = s32[4096]{0:T(1024)S(1)} fusion(s32[4096]{0:T(1024)S(1)} %get-tuple-element.17, s32[4096]{0:T(1024)S(1)} %reshape.64, s32[]{:T(128)} %constant.66.clone.1), kind=kCustom, calls=%fused_computation.42 | custom fusion | bytes 16388 | tf_op jit(solution)/shard_map/scatter | solution.py:91
  259.6 0.1 compare_and_fusion
  259.7 13.6 %all-to-all-done = bf16[128,8,512]{2,1,0:T(8,128)(2,1)S(1)} async-done(((bf16[128,8,512]{2,1,0:T(8,128)(2,1)}), bf16[128,8,512]{2,1,0:T(8,128)(2,1)S(1)}, u32[]{:S(2)}, u32[]{:S(2)}) %all-to-all-start) | async-done | bytes 1048608 | tf_op jit(solution)/shard_map/all_to_all | solution.py:82
  273.3 2.0 gather_fusion
  275.3 0.2 copy.28
  275.5 69.1 %all-reduce.2.cloned.1.call-done = bf16[512,4096]{1,0:T(8,128)(2,1)} async-done(((bf16[512,4096]{1,0:T(8,128)(2,1)}), bf16[512,4096]{1,0:T(8,128)(2,1)}) %all-reduce.2.cloned.1.call-update) | async-done | bytes 4194320 | tf_op jit(solution)/shard_map/psum | solution.py:112
  344.6 5.0 %fusion.3 = bf16[512,4096]{1,0:T(8,128)(2,1)S(1)} fusion(bf16[512,4096]{1,0:T(8,128)(2,1)} %all-gather.8.cloned.1.call-done, bf16[512,4096]{1,0:T(8,128)(2,1)} %all-reduce.2.cloned.1.call-done), kind=kLoop, calls=%fused_computation.10 | loop fusion | flops 8388608 | bytes 12582912 | tf_op jit(solution)/shard_map/convert_element_type | solution.py:113
  349.6 0.0 copy-start.3
  349.6 1.9 copy-done.3
  351.6 0.7 constant_dynamic-slice_fusion
  352.3 5.9 %multiply_reduce_fusion = (f32[512]{0:T(512)S(1)}, f32[512,512]{0,1:T(8,128)S(1)}) fusion(bf16[512,512]{0,1:T(8,128)(2,1)S(1)} %copy.28, pred[512]{0:T(512)(128)(4,1)S(1)} %get-tuple-element.15, bf16[512,4096]{1,0:T(8,128)(2,1)} %copy-done.3, bf16[4096,512]{1,0:T(8,128)(2,1)} %all-gather.14.cloned.1.call-done), kind=kOutput, calls=%fused_computation.21 | convolution fusion | flops 2148793856 | bytes 9964032 | tf_op jit(solution)/shard_map/dot_general | solution.py:117
  358.2 10.4 %psum.22 = f32[512]{0:T(512)S(1)} all-reduce(f32[512]{0:T(512)S(1)} %get-tuple-element.19), channel_id=1, replica_groups=mesh['dp'=8,'tensor_0'=4,'tensor_1'=4] {'tensor_0'}, use_global_device_ids=true, to_apply=%region_8.9 | all-reduce | flops 512 | bytes 4096 | tf_op jit(solution)/shard_map/psum | solution.py:30
  368.6 8.6 %psum.23 = f32[512]{0:T(512)S(1)} all-reduce(f32[512]{0:T(512)S(1)} %psum.22), channel_id=1, replica_groups=mesh['dp'=8,'tensor_0'=4,'tensor_1'=4] {'tensor_1'}, use_global_device_ids=true, to_apply=%region_9.10 | all-reduce | flops 512 | bytes 4096 | tf_op jit(solution)/shard_map/psum | solution.py:30
  377.2 0.6 broadcast_multiply_fusion
  377.8 1.3 copy.29
  379.1 0.0 copy-done.1
  (10 shorter events, 0.1 us)
Async XLA Ops:
  8.0 34.0 %copy-start = (bf16[512,512]{1,0:T(8,128)(2,1)S(1)}, bf16[512,512]{1,0:T(8,128)(2,1)}, u32[]{:S(2)}) copy-start(bf16[512,512]{1,0:T(8,128)(2,1)} %param.11) | copy-start | bytes 1572868
  8.0 30.4 %all-gather.6.cloned.1.call-start = ((), (), s32[]{:S(2)}) async-start(), calls=%async_computation.2 | async-start | bytes 1310720 | tf_op jit(solution)/shard_map/all_gather | solution.py:15
  8.7 86.6 %all-gather.8.cloned.1.call-start = ((), (), s32[]{:S(2)}) async-start(), calls=%async_computation.3 | async-start | bytes 5242880 | tf_op jit(solution)/shard_map/all_gather | solution.py:15
  38.4 134.9 %all-gather.10.cloned.1.call-start = ((), (), s32[]{:S(2)}) async-start(), calls=%async_computation.4 | async-start | bytes 16515072 | tf_op jit(solution)/shard_map/all_gather | solution.py:21
  41.3 179.3 %all-gather.12.cloned.1.call-start = ((), (), s32[]{:S(2)}) async-start(), calls=%async_computation.5 | async-start | bytes 8257536 | tf_op jit(solution)/shard_map/all_gather | solution.py:109
  41.9 189.0 %reduce-scatter.2.cloned.1.call-start = ((), (), s32[]{:S(2)}) async-start(), calls=%async_computation.8 | async-start | bytes 8912896 | tf_op jit(solution)/shard_map/reduce_scatter | solution.py:52
  52.1 0.7 copy-start.7
  52.1 292.5 %all-reduce.2.cloned.1.call-start = ((), (), s32[]{:S(2)}) async-start(), calls=%async_computation.6 | async-start | bytes 8388608 | tf_op jit(solution)/shard_map/psum | solution.py:112
  173.4 11.3 %copy-start.2 = (bf16[512,4096]{1,0:T(8,128)(2,1)S(1)}, bf16[512,4096]{1,0:T(8,128)(2,1)}, u32[]{:S(2)}) copy-start(bf16[512,4096]{1,0:T(8,128)(2,1)} %all-gather.8.cloned.1.call-done) | copy-start | bytes 12582916
  173.4 11.3 %copy-start.8 = (bf16[4096,1792]{1,0:T(8,128)(2,1)S(1)}, bf16[4096,1792]{1,0:T(8,128)(2,1)}, u32[]{:S(2)}) copy-start(bf16[4096,1792]{1,0:T(8,128)(2,1)} %all-gather.10.cloned.1.call-done) | copy-start | bytes 44040196
  229.8 0.7 copy-start.5
  229.8 0.7 copy-start.6
  229.8 1.2 copy-start.4
  229.8 122.5 %all-gather.14.cloned.1.call-start = ((), (), s32[]{:S(2)}) async-start(), calls=%async_computation.7 | async-start | bytes 4718592 | tf_op jit(solution)/shard_map/all_gather | solution.py:118
  234.8 38.5 %all-to-all-start = ((bf16[128,8,512]{2,1,0:T(8,128)(2,1)}), bf16[128,8,512]{2,1,0:T(8,128)(2,1)S(1)}, u32[]{:S(2)}, u32[]{:S(2)}) async-start(bf16[128,8,512]{2,1,0:T(8,128)(2,1)} %bitcast.2), calls=%async_computation.1 | async-start | bytes 2097152 | tf_op jit(solution)/shard_map/all_to_all | solution.py:82
  349.6 1.9 copy-start.3
  352.3 26.8 %copy-start.1 = (bf16[512,512]{1,0:T(8,128)(2,1)S(1)}, bf16[512,512]{1,0:T(8,128)(2,1)}, u32[]{:S(2)}) copy-start(bf16[512,512]{1,0:T(8,128)(2,1)} %param.11) | copy-start | bytes 1572868
Sparse Core Ops, SparseCore 0:
  10.5 27.8 all-gather.5
  40.1 55.2 all-gather.7
  97.1 76.2 all-gather.9
  174.9 45.7 all-gather.11
  232.0 43.3 all-gather.13
Sparse Core Ops, SparseCore 1:
  52.2 107.4 reduce-scatter.1
  229.9 114.7 all-reduce.1
where the time goes:
time: 387 us; the launch traced here: 386 us
  waiting for transfers between devices  263 us (68%)
  matrix products  43.5 us (11%)
  local copies, waits for them, and re-layouts  22.8 us (6%)
  blocking collectives  19 us (5%)
  between operations  15.4 us (4%)
  other arithmetic  13.4 us (3%)
  starting transfers between devices  9.28 us (2%)
    all_gather x1, waiting for transfers between devices, in_one_piece(): filled, at, done = (lax.all_gather(both, axis, axis=dim, tiled=True), 0, [])  74.7 us
    all_gather x2, waiting for transfers between devices, whole_of(): nearer = lax.all_gather(value, axes[-1], axis=dim, tiled=True)  72.2 us
    psum x1, waiting for transfers between devices, local(): lax.psum(partial_sum.astype(jnp.bfloat16), TENSOR).astype(jnp.float32)  69.1 us
    all_gather x1, waiting for transfers between devices, local(): lax.all_gather(w_down, 'dp', axis=1, tiled=True)  31.4 us
    psum x2, blocking collectives, one_axis_at_a_time(): value = lax.psum(value, axis)  19 us
    dot_general x2, matrix products, add_rows(): return jnp.dot(normed, portion, preferred_element_type=jnp.float32)  15.9 us
    scatter x1, local copies, waits for them, and re-layouts, local(): jnp.zeros(dest_row.shape, jnp.int32).at[dest_row].set(arrival_index)  15.8 us
    all_to_all x1, waiting for transfers between devices, local(): lax.all_to_all(send_blocks.reshape(source_count, capacity, col_width), DP...  13.6 us
  transfers between devices with their start and end apart: 8, of which 6 were waited for; matrix products, arithmetic and copies ran while one was open for 18% of the time, Pallas kernels for 0%

commit v1 on v0

v1 whole, which is shorter than its diff:
```python
import functools
import jax
import jax.numpy as jnp
from jax import lax
from jax.sharding import Mesh
from jax.sharding import PartitionSpec as P
from jax.experimental import pallas as pl
from jax.experimental.pallas import tpu as pltpu

HT = 8192
BF = jnp.bfloat16
F32 = jnp.float32
AXES = ("x", "c", "z", "y")
TENSOR = ("z", "y")
DP = ("x", "c")


class Net:
    def __init__(self, send_sems, recv_sems):
        self.ss, self.rs, self.made = send_sems, recv_sems, {}

    def send(self, role, src, dst, dev):
        i = len(self.made)
        cp = pltpu.make_async_remote_copy(
            src_ref=src,
            dst_ref=dst,
            send_sem=self.ss.at[i],
            recv_sem=self.rs.at[i],
            device_id=dev,
            device_id_type=pl.DeviceIdType.MESH,
        )
        cp.start()
        self.made[role] = cp

    def got(self, *roles):
        for role in roles:
            self.made[role].wait_recv()

    def drain(self):
        for cp in self.made.values():
            cp.wait_send()


def greet(partners):
    barrier = pltpu.get_barrier_semaphore()
    for dev in partners:
        pl.semaphore_signal(barrier, inc=1, device_id=dev, device_id_type=pl.DeviceIdType.MESH)
    pl.semaphore_wait(barrier, len(partners))


N1 = 68


def first_kernel(
    attn, wout_hbm, resid, sin, gain, wg_hbm, wu_hbm,
    hid, th, xrow,
    w1, xg, nrm, wout, part, rp, rq, sp, sq, rp2, rq2, acc, tmp, loc, wsem, ss, rs,
):
    x, c, z, y = (lax.axis_index(a) for a in AXES)
    t = z * 4 + y
    d = x * 2 + c

    def at(base, k):
        return lax.rem(base + k, 4)

    xr, xl, xo = at(x, 1), at(x, 3), at(x, 2)
    sib = {"c": 1 - c}
    right, left = {"x": xr}, {"x": xl}
    loads = []
    for h in range(2):
        rows = pl.ds(h * 256, 256)
        loads.append(pltpu.make_async_copy(wg_hbm.at[rows], w1.at[d, h, :, pl.ds(0, 896)], loc.at[2 * h]))
        loads.append(pltpu.make_async_copy(wu_hbm.at[rows], w1.at[d, h, :, pl.ds(896, 896)], loc.at[2 * h + 1]))
    loads.append(pltpu.make_async_copy(sin, xg.at[z, y], loc.at[4]))
    for cp in loads:
        cp.start()
    wloads = [
        pltpu.make_async_copy(wout_hbm.at[:, pl.ds(b * 512, 512)], wout.at[b], wsem.at[b]) for b in range(16)
    ]
    for cp in wloads:
        cp.start()

    greet(
        [sib, right, left]
        + [{"y": at(y, k)} for k in (1, 2, 3)]
        + [{"z": at(z, k)} for k in (1, 2, 3)]
    )
    net = Net(ss, rs)

    def piece(who, half):
        return pl.ds(who * 256 + half * 128, 128)

    def ring_open(tag, axis, base, ref):
        up, down = {axis: at(base, 1)}, {axis: at(base, 3)}
        net.send(tag + "LA", ref(0, 0), ref(0, 0), up)
        net.send(tag + "RB", ref(0, 1), ref(0, 1), down)
        net.send(tag + "LB", ref(0, 1), ref(0, 1), up)
        net.send(tag + "RA", ref(0, 0), ref(0, 0), down)

    def ring_forward(tag, axis, base, ref):
        up, down = {axis: at(base, 1)}, {axis: at(base, 3)}
        net.got(tag + "LA")
        net.send(tag + "OA", ref(3, 0), ref(3, 0), up)
        net.got(tag + "RB")
        net.send(tag + "OB", ref(1, 1), ref(1, 1), down)

    def ring_close(tag):
        net.got(tag + "LB", tag + "RA", tag + "OA", tag + "OB")

    p1 = lambda k, h: xg.at[z, at(y, k), piece(0, h)]
    q1 = lambda k, h: xg.at[at(z, k), y, piece(1, h)]
    p2 = lambda k, h: xg.at[at(z, k), :, piece(0, h)]
    q2 = lambda k, h: xg.at[:, at(y, k), piece(1, h)]

    loads[4].wait()
    ring_open("p1", "y", y, p1)
    ring_open("q1", "z", z, q1)
    for cp in loads[:4]:
        cp.wait()
    net.send("wLA", w1.at[d, 0], w1.at[d, 0], right)
    net.send("wRB", w1.at[d, 1], w1.at[d, 1], left)
    net.send("wLB", w1.at[d, 1], w1.at[d, 1], right)
    net.send("wRA", w1.at[d, 0], w1.at[d, 0], left)
    net.send("sIA", w1.at[d, 0], w1.at[d, 0], sib)
    net.send("sIB", w1.at[d, 1], w1.at[d, 1], sib)

    mine = pl.ds(pl.multiple_of(t * 32, 32), 32)

    def partial(b):
        wloads[b].wait()
        tmp[...] = jnp.dot(attn[...], wout[b], preferred_element_type=F32)
        tmp[mine, :] += resid[:, b * 512:(b + 1) * 512].astype(F32)
        part[b] = tmp[...].astype(BF)

    partial(0)
    partial(1)
    partial(2)
    partial(3)
    ring_forward("p1", "y", y, p1)
    ring_forward("q1", "z", z, q1)
    partial(4)
    partial(5)
    ring_close("p1")
    ring_open("p2", "z", z, p2)
    ring_close("q1")
    ring_open("q2", "y", y, q2)
    for b in range(6, 16):
        partial(b)
    ring_forward("p2", "z", z, p2)
    ring_forward("q2", "y", y, q2)

    P_ROWS, Q_ROWS = pl.ds(0, 256), pl.ds(256, 256)
    for k in (1, 2, 3, 0):
        for j in (1, 2, 3):
            zz, yy = at(z, k), at(y, j)
            net.send(f"tp{k}{j}", part.at[zz * 4 + yy, P_ROWS], rp.at[j - 1, k], {"y": yy})
            zz, yy = at(z, j), at(y, k)
            net.send(f"tq{k}{j}", part.at[zz * 4 + yy, Q_ROWS], rq.at[j - 1, k], {"z": zz})

    ring_close("p2")
    ring_close("q2")
    xrow[...] = xg[:, :, mine, :].reshape(16, 32, 256)

    @pl.loop(0, 4)
    def _(r):
        rows = pl.ds(pl.multiple_of(r * 128, 128), 128)
        total = jnp.zeros((128, 256), F32)
        for s in range(16):
            v = xg[s // 4, s % 4, rows, :].astype(F32)
            total = total + v * v
        scale = lax.rsqrt(jnp.sum(total, axis=1, keepdims=True) / 4096.0 + 1e-05)
        for s in range(16):
            v = xg[s // 4, s % 4, rows, :].astype(F32)
            nrm[s, rows, :] = (v * scale * gain[s:s + 1, :].astype(F32)).astype(BF)

    def gate_up(slots, first):
        @pl.loop(0, 7)
        def _(j):
            cols = pl.ds(pl.multiple_of(j * 256, 256), 256)
            total = None
            for s, h in slots:
                term = jnp.dot(nrm[s * 2 + h], w1[s, h, :, cols], preferred_element_type=F32)
                total = term if total is None else total + term
            if first:
                acc[:, cols] = total
            else:
                acc[:, cols] += total

    def slot(xx, cc):
        return xx * 2 + cc

    def pass_on(role, s, h):
        net.send(role, w1.at[s, h], w1.at[s, h], sib)

    net.got("wLA")
    net.send("wOA", w1.at[slot(xl, c), 0], w1.at[slot(xl, c), 0], right)
    pass_on("sLA", slot(xl, c), 0)
    net.got("wRB")
    net.send("wOB", w1.at[slot(xr, c), 1], w1.at[slot(xr, c), 1], left)
    pass_on("sRB", slot(xr, c), 1)
    net.got("sIA", "sIB")
    gate_up([(d, 0), (d, 1), (slot(x, 1 - c), 0), (slot(x, 1 - c), 1)], True)
    net.got("sLA", "sRB")
    gate_up([(slot(xl, c), 0), (slot(xr, c), 1), (slot(xl, 1 - c), 0), (slot(xr, 1 - c), 1)], False)

    def reduce_p(k):
        net.got(f"tp{k}1", f"tp{k}2", f"tp{k}3")
        zz = at(z, k)
        s = part[zz * 4 + y, :256, :].astype(F32)
        for j in range(3):
            s = s + rp[j, k].astype(F32)
        if k == 0:
            th[:256, :] = s
        else:
            sp[k - 1] = s.astype(BF)
            net.send(f"up{k}", sp.at[k - 1], rp2.at[k - 1], {"z": zz})

    def reduce_q(k):
        net.got(f"tq{k}1", f"tq{k}2", f"tq{k}3")
        yy = at(y, k)
        s = part[z * 4 + yy, 256:, :].astype(F32)
        for j in range(3):
            s = s + rq[j, k].astype(F32)
        if k == 0:
            th[256:, :] = s
        else:
            sq[k - 1] = s.astype(BF)
            net.send(f"uq{k}", sq.at[k - 1], rq2.at[k - 1], {"y": yy})

    reduce_p(1)
    reduce_q(1)
    net.got("wLB")
    pass_on("sLB", slot(xl, c), 1)
    net.got("wRA")
    pass_on("sRA", slot(xr, c), 0)
    net.got("sLB", "sRA")
    gate_up([(slot(xl, c), 1), (slot(xr, c), 0), (slot(xl, 1 - c), 1), (slot(xr, 1 - c), 0)], False)
    reduce_p(2)
    reduce_q(2)
    net.got("wOA")
    pass_on("sOA", slot(xo, c), 0)
    net.got("wOB")
    pass_on("sOB", slot(xo, c), 1)
    reduce_p(3)
    reduce_q(3)
    net.got("sOA", "sOB")
    gate_up([(slot(xo, c), 0), (slot(xo, c), 1), (slot(xo, 1 - c), 0), (slot(xo, 1 - c), 1)], False)

    @pl.loop(0, 7)
    def _(j):
        g = acc[:, pl.ds(pl.multiple_of(j * 128, 128), 128)]
        u = acc[:, pl.ds(pl.multiple_of(896 + j * 128, 128), 128)]
        hid[:, pl.ds(pl.multiple_of(j * 128, 128), 128)] = (jax.nn.silu(g) * u).astype(BF)

    reduce_p(0)
    reduce_q(0)
    for k in (1, 2, 3):
        net.got(f"up{k}")
        th[:256, :] += rp2[k - 1].astype(F32)
        net.got(f"uq{k}")
        th[256:, :] += rq2[k - 1].astype(F32)
    net.drain()


def call_first(attn, wout, resid, sin, gain, wg, wu):
    vm = pl.BlockSpec(memory_space=pltpu.VMEM)
    hb = pl.BlockSpec(memory_space=pl.ANY)
    return pl.pallas_call(
        first_kernel,
        name="first",
        out_shape=(
            jax.ShapeDtypeStruct((512, 896), BF),
            jax.ShapeDtypeStruct((512, 512), F32),
            jax.ShapeDtypeStruct((16, 32, 256), BF),
        ),
        in_specs=[vm, hb, vm, vm, vm, hb, hb],
        out_specs=(vm, vm, vm),
        scratch_shapes=[
            pltpu.VMEM((8, 2, 256, 1792), BF),
            pltpu.VMEM((4, 4, 512, 256), BF),
            pltpu.VMEM((16, 512, 256), BF),
            pltpu.VMEM((16, 512, 512), BF),
            pltpu.VMEM((16, 512, 512), BF),
            pltpu.VMEM((3, 4, 256, 512), BF),
            pltpu.VMEM((3, 4, 256, 512), BF),
            pltpu.VMEM((3, 256, 512), BF),
            pltpu.VMEM((3, 256, 512), BF),
            pltpu.VMEM((3, 256, 512), BF),
            pltpu.VMEM((3, 256, 512), BF),
            pltpu.VMEM((512, 1792), F32),
            pltpu.VMEM((512, 512), F32),
            pltpu.SemaphoreType.DMA((5,)),
            pltpu.SemaphoreType.DMA((16,)),
            pltpu.SemaphoreType.DMA((N1,)),
            pltpu.SemaphoreType.DMA((N1,)),
        ],
        compiler_params=pltpu.CompilerParams(
            collective_id=0, has_side_effects=True, vmem_limit_bytes=67043328
        ),
    )(attn, wout, resid, sin, gain, wg, wu)


def one_axis_at_a_time(value, axes):
    for axis in axes:
        value = lax.psum(value, axis)
    return value


def local(
    attn_ctx,
    w_out,
    resid,
    teacher_gain,
    dest_row,
    student_in,
    student_gain,
    w_gate,
    w_up,
    w_down,
    proj,
):
    t = lax.axis_index(TENSOR)
    d = lax.axis_index(DP)
    hidden, th, xrow = call_first(
        attn_ctx, w_out, resid, student_in, student_gain.reshape(16, 256), w_gate, w_up
    )
    ssq = lax.psum(jnp.sum(th * th, axis=1), TENSOR)
    gain = lax.dynamic_slice_in_dim(teacher_gain, t * 512, 512, 0).astype(F32)
    final = (th * lax.rsqrt(ssq / HT + 1e-06)[:, None] * gain[None, :]).astype(BF)
    everyone = lax.all_gather(final, DP, axis=0, tiled=True)
    pick = (dest_row[None, :] == (d * 512 + jnp.arange(512))[:, None]).astype(BF)
    target = jnp.dot(pick, everyone, preferred_element_type=F32)
    partial_sum = jnp.dot(
        hidden, lax.all_gather(w_down, DP, axis=1, tiled=True), preferred_element_type=F32
    )
    rows = lax.psum_scatter(partial_sum.astype(BF), TENSOR, scatter_dimension=0, tiled=True).astype(F32)
    out_rows = (rows + xrow.transpose(1, 0, 2).reshape(32, 4096).astype(F32)).astype(BF)
    out_full = lax.all_gather(out_rows, TENSOR, axis=0, tiled=True)
    out_local = lax.dynamic_slice_in_dim(out_full, t * 256, 256, 1)
    pred = jnp.dot(
        out_full, lax.all_gather(proj, DP, axis=0, tiled=True), preferred_element_type=F32
    )
    residue = pred - target
    row_loss = one_axis_at_a_time(jnp.sum(residue * residue, axis=1), TENSOR) / HT
    return (out_local, row_loss, residue)


def solution(mesh):
    torus = Mesh(mesh.devices.reshape(4, 2, 4, 4), AXES)
    in_specs = (
        P(DP, TENSOR),
        P(TENSOR, None),
        P(DP + TENSOR, None),
        P(),
        P(),
        P(DP, TENSOR),
        P(),
        P(DP, TENSOR),
        P(DP, TENSOR),
        P(TENSOR, DP),
        P(DP, TENSOR),
    )
    out_specs = (P(DP, TENSOR), P(DP), P(DP, TENSOR))
    return jax.shard_map(local, mesh=torus, in_specs=in_specs, out_specs=out_specs, check_vma=False)
```

time: 387 us -> 361 us (0.933)
  waiting for transfers between devices: 263 us -> 150 us
  Pallas kernels: 0 us -> 107 us
  blocking collectives: 19 us -> 59.3 us
  matrix products: 43.5 us -> 20.6 us
  local copies, waits for them, and re-layouts: 22.8 us -> 4.46 us
  other arithmetic: 13.4 us -> 4.19 us
  starting transfers between devices: 9.28 us -> 0.38 us
    pallas_call x0 -> x1, Pallas kernels: none -> 107 us  [call_first(): pl.pallas_call(first_kernel, name='first', out_shape=(jax.ShapeDtypeStruc...]
    all_gather x5 -> x4, waiting for transfers between devices: 178 us -> 73 us  [the longest x1 45.1 us: local(): out_full = lax.all_gather(out_rows, TENSOR, axis=0, tiled=True)]
    reduce_scatter x1, waiting for transfers between devices: 0.02 us -> 76.2 us  [local(): lax.psum_scatter(partial_sum.astype(BF), TENSOR, scatter_dimension=0, til...]
    psum x1 -> x0, waiting for transfers between devices: 69.1 us -> none  [local(): lax.psum(partial_sum.astype(jnp.bfloat16), TENSOR).astype(jnp.float32)]
    psum x0 -> x1, blocking collectives: none -> 38.1 us  [local(): ssq = lax.psum(jnp.sum(th * th, axis=1), TENSOR)]
    dot_general x6 -> x3, matrix products: 43.5 us -> 20.6 us  [the longest x1 9.98 us: local(): jnp.dot(hidden, lax.all_gather(w_down, DP, axis=1, tiled=True), preferred...]
    scatter x1 -> x0, local copies, waits for them, and re-layouts: 15.8 us -> none  [local(): jnp.zeros(dest_row.shape, jnp.int32).at[dest_row].set(arrival_index)]
    all_to_all x1 -> x0, waiting for transfers between devices: 13.6 us -> none  [local(): lax.all_to_all(send_blocks.reshape(source_count, capacity, col_width), DP...]
  transfers between devices with their start and end apart: 8 -> 5, of which waited for: 6 -> 3; matrix products, arithmetic and copies ran while one was open for 18% -> 3% of each run, Pallas kernels for 0% -> 30%
where the time goes in v1:
time: 361 us
  waiting for transfers between devices  150 us (42%)
  Pallas kernels  107 us (30%)
  blocking collectives  59.3 us (16%)
  matrix products  20.6 us (6%)
  between operations  13.9 us (4%)
  local copies, waits for them, and re-layouts  4.46 us (1%)
  other arithmetic  4.19 us (1%)
    pallas_call x1, Pallas kernels, call_first(): pl.pallas_call(first_kernel, name='first', out_shape=(jax.ShapeDtypeStruc...  107 us
    reduce_scatter x1, waiting for transfers between devices, local(): lax.psum_scatter(partial_sum.astype(BF), TENSOR, scatter_dimension=0, til...  76.2 us
    all_gather x1, waiting for transfers between devices, local(): out_full = lax.all_gather(out_rows, TENSOR, axis=0, tiled=True)  45.1 us
    psum x1, blocking collectives, local(): ssq = lax.psum(jnp.sum(th * th, axis=1), TENSOR)  38.1 us
    all_gather x1, waiting for transfers between devices, local(): everyone = lax.all_gather(final, DP, axis=0, tiled=True)  27.9 us
    psum x2, blocking collectives, one_axis_at_a_time(): value = lax.psum(value, axis)  21.1 us
    dot_general x1, matrix products, local(): jnp.dot(hidden, lax.all_gather(w_down, DP, axis=1, tiled=True), preferred...  9.98 us
  transfers between devices with their start and end apart: 5, of which 3 were waited for; matrix products, arithmetic and copies ran while one was open for 3% of the time, Pallas kernels for 30%

profile of v1, /device:TPU:0, one launch (start us, length us, event | category | flops | bytes accessed | tf_op | source)
XLA Modules:
  0.0 360.7 jit_solution(18334068346631182405)
XLA Ops:
  7.2 0.0 all-gather.5.cloned.1.call-start
  7.2 0.7 all-gather.5.cloned.1.call-update
  7.9 0.0 reduce-scatter.2.cloned.1.call-start
  7.9 1.3 reshape.19.gain
  9.2 107.5 %first.1 = (bf16[512,896]{1,0:T(8,128)(2,1)}, f32[512,512]{1,0:T(8,128)}, bf16[16,32,256]{2,1,0:T(8,128)(2,1)}) custom-call(bf16[512,512]{1,0:T(8,128)(2,1)} %attn.1, bf16[512,8192]{1,0:T(8,128)(2,1)} %wout_hbm.1, bf16[32,8192]{1,0:T(8,128)(2,1)} %resid.1, bf16[512,256]{1,0:T(8,128)(2,1)} %sin.1, bf16[16,256]{1,0:T(8,128)(2,1)} %reshape.19.gain, ...), custom_call_target="tpu_custom_call" | custom-call | tf_op jit(solution)/shard_map/first/pallas_call | solution.py:268
  116.8 0.0 all-gather.5.cloned.1.call-done
  116.8 10.0 %convolution_convert_fusion = bf16[512,4096]{1,0:T(8,128)(2,1)} fusion(bf16[512,896]{1,0:T(8,128)(2,1)} %get-tuple-element.6, bf16[896,4096]{1,0:T(8,128)(2,1)} %all-gather.5.cloned.1.call-done), kind=kOutput, calls=%fused_computation.2 | convolution fusion | flops 3760193536 | bytes 12451840 | tf_op jit(solution)/shard_map/dot_general | solution.py:333
  126.8 0.0 copy-start.1
  126.8 0.0 copy-start
  126.8 0.0 reduce-scatter.2.cloned.1.call-update
  126.8 0.2 all-gather.9.cloned.1.call-start
  127.0 0.5 all-gather.9.cloned.1.call-update
  127.5 0.0 all-gather.7.cloned.1.call-start
  127.6 0.1 copy-done.1
  127.8 76.2 %reduce-scatter.2.cloned.1.call-done = bf16[32,4096]{1,0:T(8,128)(2,1)} async-done(((bf16[512,4096]{1,0:T(8,128)(2,1)}), bf16[32,4096]{1,0:T(8,128)(2,1)}) %reduce-scatter.2.cloned.1.call-update) | async-done | bytes 262160 | tf_op jit(solution)/shard_map/reduce_scatter | solution.py:336
  204.0 1.7 add_convert_fusion
  205.7 0.0 all-gather.7.cloned.1.call-update
  205.8 0.0 all-gather.11.cloned.1.call-start
  205.8 0.0 copy-done
  205.8 0.1 multiply_reduce_fusion.1
  206.0 38.1 %psum.21 = f32[512]{0:T(512)S(1)} all-reduce(f32[512]{0:T(512)S(1)} %multiply_reduce_fusion.1), channel_id=1, replica_groups=mesh['x'=4,'c'=2,'z'=4,'y'=4] {'z','y'}, use_global_device_ids=true, to_apply=%region_2.0 | all-reduce | flops 512 | bytes 4096 | tf_op jit(solution)/shard_map/psum | solution.py:327
  244.1 0.8 dynamic-slice_convert_fusion
  244.9 1.0 multiply_convert_fusion
  245.8 0.0 all-gather.11.cloned.1.call-update
  245.9 0.0 copy-start.2
  245.9 0.0 all-gather.9.cloned.1.call-done
  245.9 45.1 %all-gather.7.cloned.1.call-done = bf16[512,4096]{1,0:T(8,128)(2,1)} async-done(((bf16[32,4096]{1,0:T(8,128)(2,1)}), bf16[512,4096]{1,0:T(8,128)(2,1)}) %all-gather.7.cloned.1.call-update) | async-done | bytes 4194320 | tf_op jit(solution)/shard_map/all_gather | solution.py:338
  291.0 5.8 %fusion.7 = f32[512,512]{0,1:T(8,128)S(1)} fusion(bf16[512,4096]{1,0:T(8,128)(2,1)} %all-gather.7.cloned.1.call-done, bf16[4096,512]{1,0:T(8,128)(2,1)} %all-gather.9.cloned.1.call-done), kind=kOutput, calls=%fused_computation.16 | convolution fusion | flops 2147483648 | bytes 9437184 | tf_op jit(solution)/shard_map/dot_general | solution.py:340
  296.8 27.9 %all-gather.11.cloned.1.call-done = bf16[4096,512]{1,0:T(8,128)(2,1)} async-done(((bf16[512,512]{1,0:T(8,128)(2,1)}), bf16[4096,512]{1,0:T(8,128)(2,1)}) %all-gather.11.cloned.1.call-update) | async-done | bytes 4194320 | tf_op jit(solution)/shard_map/all_gather | solution.py:330
  324.7 0.0 copy-done.2
  324.7 4.7 %multiply_reduce_fusion = (f32[512]{0:T(512)S(1)}, f32[512,512]{0,1:T(8,128)S(1)}) fusion(f32[512,512]{0,1:T(8,128)S(1)} %fusion.7, bf16[4096,512]{1,0:T(8,128)(2,1)} %all-gather.11.cloned.1.call-done, s32[4096]{0:T(1024)S(1)} %copy-done.2, s32[512]{0:T(512)S(1)} %iota_add_fusion), kind=kOutput, calls=%fused_computation.6 | convolution fusion | flops 2150366720 | bytes 6311936 | tf_op jit(solution)/shard_map/dot_general | solution.py:332
  329.5 10.7 %psum.22 = f32[512]{0:T(512)S(1)} all-reduce(f32[512]{0:T(512)S(1)} %get-tuple-element.15), channel_id=1, replica_groups=mesh['x'=4,'c'=2,'z'=4,'y'=4] {'z'}, use_global_device_ids=true, to_apply=%region_4.0 | all-reduce | flops 512 | bytes 4096 | tf_op jit(solution)/shard_map/psum | solution.py:305
  340.2 10.5 %psum.23 = f32[512]{0:T(512)S(1)} all-reduce(f32[512]{0:T(512)S(1)} %psum.22), channel_id=1, replica_groups=mesh['x'=4,'c'=2,'z'=4,'y'=4] {'y'}, use_global_device_ids=true, to_apply=%region_5.0 | all-reduce | flops 512 | bytes 4096 | tf_op jit(solution)/shard_map/psum | solution.py:305
  350.6 0.6 broadcast_multiply_fusion
  351.2 1.3 copy.16
  352.5 1.7 constant_dynamic-slice_fusion
  (4 shorter events, 0.1 us)
Async XLA Ops:
  7.2 109.6 %all-gather.5.cloned.1.call-start = ((), (), s32[]{:S(2)}) async-start(), calls=%async_computation.1 | async-start | bytes 8257536 | tf_op jit(solution)/shard_map/all_gather | solution.py:334
  7.9 196.2 %reduce-scatter.2.cloned.1.call-start = ((), (), s32[]{:S(2)}) async-start(), calls=%async_computation.2 | async-start | bytes 4456448 | tf_op jit(solution)/shard_map/reduce_scatter | solution.py:336
  126.8 0.9 copy-start.1
  126.8 79.1 %copy-start = (f32[512,512]{1,0:T(8,128)S(1)}, f32[512,512]{1,0:T(8,128)}, u32[]{:S(2)}) copy-start(f32[512,512]{1,0:T(8,128)} %get-tuple-element.8) | copy-start | bytes 3145732
  126.8 119.1 %all-gather.9.cloned.1.call-start = ((), (), s32[]{:S(2)}) async-start(), calls=%async_computation.4 | async-start | bytes 4718592 | tf_op jit(solution)/shard_map/all_gather | solution.py:341
  127.5 163.4 %all-gather.7.cloned.1.call-start = ((), (), s32[]{:S(2)}) async-start(), calls=%async_computation.3 | async-start | bytes 4456448 | tf_op jit(solution)/shard_map/all_gather | solution.py:338
  205.8 119.0 %all-gather.11.cloned.1.call-start = ((), (), s32[]{:S(2)}) async-start(), calls=%async_computation.5 | async-start | bytes 4718592 | tf_op jit(solution)/shard_map/all_gather | solution.py:330
  245.9 78.9 %copy-start.2 = (s32[4096]{0:T(1024)S(1)}, s32[4096]{0:T(1024)}, u32[]{:S(2)}) copy-start(s32[4096]{0:T(1024)} %param.15) | copy-start | bytes 49156
Sparse Core Ops, SparseCore 0:
  9.7 77.2 all-gather.4
  126.9 77.0 reduce-scatter.1
  205.8 31.0 all-gather.8
  239.5 51.4 all-gather.6
  293.1 31.5 all-gather.10

commit v2 on v1

--- a/solution.py
+++ b/solution.py
@@ -300,10 +300,338 @@
     )(attn, wout, resid, sin, gain, wg, wu)
 
 
-def one_axis_at_a_time(value, axes):
-    for axis in axes:
-        value = lax.psum(value, axis)
-    return value
+N2 = 174
+
+
+def second_kernel(
+    hid, wd_hbm, pj_hbm, xrow, th, tgain, dest,
+    out, res, loss,
+    w2, pj, tg, pt, so, r1, s1, r2, stat_y, stat_z, stat_s, loss_y, loss_z, loss_s, loc, ss, rs,
+):
+    x, c, z, y = (lax.axis_index(a) for a in AXES)
+    t = z * 4 + y
+    d = x * 2 + c
+
+    def at(base, k):
+        return lax.rem(base + k, 4)
+
+    xr, xl, xo = at(x, 1), at(x, 3), at(x, 2)
+    sib = {"c": 1 - c}
+    right, left = {"x": xr}, {"x": xl}
+    w2_loads, pj_loads = [], []
+    for h in range(2):
+        w2_loads.append(pltpu.make_async_copy(wd_hbm.at[:, pl.ds(h * 256, 256)], w2.at[d, h], loc.at[h]))
+        pj_loads.append(pltpu.make_async_copy(pj_hbm.at[pl.ds(h * 256, 256)], pj.at[d, h], loc.at[2 + h]))
+    for cp in w2_loads + pj_loads:
+        cp.start()
+    greet(
+        [sib, right, left]
+        + [{"y": at(y, k)} for k in (1, 2, 3)]
+        + [{"z": at(z, k)} for k in (1, 2, 3)]
+    )
+    net = Net(ss, rs)
+    owner = {"I": x, "L": xl, "R": xr, "O": xo}
+    half = {"A": 0, "B": 1}
+
+    def shard(role, core):
+        return owner[role[0]] * 2 + core, half[role[1]]
+
+    def along_x_open(tag, buf):
+        net.send(tag + "LA", buf.at[d, 0], buf.at[d, 0], right)
+        net.send(tag + "RB", buf.at[d, 1], buf.at[d, 1], left)
+        net.send(tag + "LB", buf.at[d, 1], buf.at[d, 1], right)
+        net.send(tag + "RA", buf.at[d, 0], buf.at[d, 0], left)
+        net.send(tag + "sIA", buf.at[d, 0], buf.at[d, 0], sib)
+        net.send(tag + "sIB", buf.at[d, 1], buf.at[d, 1], sib)
+
+    def along_x_take(tag, buf, role):
+        ref = buf.at[shard(role, c)]
+        net.got(tag + role)
+        if role == "LA":
+            net.send(tag + "OA", ref, ref, right)
+        if role == "RB":
+            net.send(tag + "OB", ref, ref, left)
+        net.send(tag + "s" + role, ref, ref, sib)
+
+    groups = (("IA", "IB"), ("LA", "RB"), ("LB", "RA"), ("OA", "OB"))
+
+    def partial(g, pq):
+        core = c if pq == 0 else 1 - c
+        for i in range(2):
+            term = jnp.dot(hid[...], w2[shard(groups[g][i], core)], preferred_element_type=F32)
+            pt[g, pq, :, :, :, i * 256:(i + 1) * 256] = term.astype(BF).reshape(4, 4, 32, 256)
+        for j in (1, 2, 3):
+            if pq == 0:
+                yy = at(y, j)
+                net.send(f"a{g}0{j}", pt.at[g, 0, :, yy], r1.at[g, 0, j - 1], {"y": yy})
+            else:
+                zz = at(z, j)
+                net.send(f"a{g}1{j}", pt.at[g, 1, zz], r1.at[g, 1, j - 1], {"z": zz})
+
+    own_sum = {}
+
+    def middle(g, pq):
+        net.got(*[f"a{g}{pq}{j}" for j in (1, 2, 3)])
+        for k in (1, 2, 3, 0):
+            other = at(z if pq == 0 else y, k)
+            mine = pt[g, 0, other, y] if pq == 0 else pt[g, 1, z, other]
+            s = mine.astype(F32)
+            for j in range(3):
+                s = s + r1[g, pq, j, other].astype(F32)
+            if k == 0:
+                own_sum[g, pq] = s
+            else:
+                s1[g, pq, k - 1] = s.astype(BF)
+                dev = {"z": other} if pq == 0 else {"y": other}
+                net.send(f"b{g}{pq}{k}", s1.at[g, pq, k - 1], r2.at[g, pq, k - 1], dev)
+
+    def finish(g, pq):
+        net.got(*[f"b{g}{pq}{j}" for j in (1, 2, 3)])
+        s = own_sum[g, pq]
+        for j in range(3):
+            s = s + r2[g, pq, j].astype(F32)
+        core = c if pq == 0 else 1 - c
+        for i in range(2):
+            dd, h = shard(groups[g][i], core)
+            xin = xrow[dd * 2 + h].astype(F32)
+            so[g, pq, z, y, :, i * 256:(i + 1) * 256] = (xin + s[:, i * 256:(i + 1) * 256]).astype(BF)
+        ref = so.at[g, pq, z, y]
+        for j in (1, 2, 3):
+            dev = {"y": at(y, j)} if pq == 0 else {"z": at(z, j)}
+            net.send(f"c{g}{pq}{j}", ref, ref, dev)
+
+    def spread_parts(g, pq):
+        if pq == 0:
+            return "z", z, lambda k, h: so.at[g, 0, at(z, k), pl.ds(2 * h, 2)]
+        return "y", y, lambda k, h: so.at[g, 1, pl.ds(2 * h, 2), at(y, k)]
+
+    def spread_open(g, pq):
+        net.got(*[f"c{g}{pq}{j}" for j in (1, 2, 3)])
+        axis, base, ref = spread_parts(g, pq)
+        tag = f"d{g}{pq}"
+        up, down = {axis: at(base, 1)}, {axis: at(base, 3)}
+        net.send(tag + "LA", ref(0, 0), ref(0, 0), up)
+        net.send(tag + "RB", ref(0, 1), ref(0, 1), down)
+        net.send(tag + "LB", ref(0, 1), ref(0, 1), up)
+        net.send(tag + "RA", ref(0, 0), ref(0, 0), down)
+
+    def spread_forward(g, pq):
+        axis, base, ref = spread_parts(g, pq)
+        tag = f"d{g}{pq}"
+        net.got(tag + "LA")
+        net.send(tag + "OA", ref(3, 0), ref(3, 0), {axis: at(base, 1)})
+        net.got(tag + "RB")
+        net.send(tag + "OB", ref(1, 1), ref(1, 1), {axis: at(base, 3)})
+
+    def spread_close(g, pq):
+        tag = f"d{g}{pq}"
+        net.got(tag + "LB", tag + "RA", tag + "OA", tag + "OB")
+
+    def predict(g):
+        spread_close(g, 0)
+        spread_close(g, 1)
+        for pq in range(2):
+            core = c if pq == 0 else 1 - c
+            left_side = so[g, pq].reshape(512, 512)
+            total = None
+            for i in range(2):
+                term = jnp.dot(
+                    left_side[:, i * 256:(i + 1) * 256],
+                    pj[shard(groups[g][i], core)],
+                    preferred_element_type=F32,
+                )
+                total = term if total is None else total + term
+            if g == 0 and pq == 0:
+                res[...] = total
+            else:
+                res[...] += total
+
+    def row_squares(value):
+        v = value * value
+        v = v[:, 0:128] + v[:, 128:256] + v[:, 256:384] + v[:, 384:512]
+        v = v.T
+        parts = v[0:8, :]
+        for i in range(1, 16):
+            parts = parts + v[8 * i:8 * i + 8, :]
+        return parts
+
+    def stat_open(tag, own, inbox, axis, base):
+        for j in (1, 2, 3):
+            net.send(f"{tag}{j}", own, inbox.at[j - 1], {axis: at(base, j)})
+
+    def stat_take(tag, own, inbox):
+        net.got(*[f"{tag}{j}" for j in (1, 2, 3)])
+        return own[...] + inbox[0] + inbox[1] + inbox[2]
+
+    def landed(g):
+        return target_of(groups[g], c) + target_of(groups[g], 1 - c)
+
+    def target_of(roles, core):
+        return [shard(r, core) for r in roles]
+
+    row_id = d * 512 + lax.broadcasted_iota(jnp.int32, (512, 256), 0)
+
+    def subtract_target(slots):
+        total = None
+        for dd, h in slots:
+            pick = dest[dd * 2 + h]
+            onehot = jnp.where(row_id == pick, 1.0, 0.0).astype(BF)
+            term = jnp.dot(onehot, tg[dd, h], preferred_element_type=F32)
+            total = term if total is None else total + term
+        res[...] -= total
+
+    stat_s[0] = row_squares(th[...])
+    stat_open("ty", stat_s.at[0], stat_y, "y", y)
+    for cp in w2_loads:
+        cp.wait()
+    along_x_open("w", w2)
+    partial(0, 0)
+    stat_s[1] = stat_take("ty", stat_s.at[0], stat_y)
+    stat_open("tz", stat_s.at[1], stat_z, "z", z)
+    net.got("wsIA", "wsIB")
+    partial(0, 1)
+    total = jnp.sum(stat_take("tz", stat_s.at[1], stat_z), axis=0, keepdims=True)
+    scale = jnp.broadcast_to(lax.rsqrt(total / HT + 1e-06), (128, 512)).T
+    gain = tgain[t].astype(F32)
+    for h in range(2):
+        for i in range(4):
+            rows, cols = slice(h * 256, h * 256 + 256), slice(i * 128, i * 128 + 128)
+            tg[d, h, :, cols] = (th[rows, cols] * scale[rows, :] * gain[:, cols]).astype(BF)
+    middle(0, 0)
+    middle(0, 1)
+    finish(0, 0)
+    finish(0, 1)
+    along_x_take("w", w2, "LA")
+    along_x_take("w", w2, "RB")
+    partial(1, 0)
+    spread_open(0, 0)
+    spread_open(0, 1)
+    net.got("wsLA", "wsRB")
+    partial(1, 1)
+    for cp in pj_loads:
+        cp.wait()
+    along_x_open("p", pj)
+    middle(1, 0)
+    middle(1, 1)
+    spread_forward(0, 0)
+    spread_forward(0, 1)
+    finish(1, 0)
+    finish(1, 1)
+    along_x_take("w", w2, "LB")
+    along_x_take("w", w2, "RA")
+    partial(2, 0)
+    spread_open(1, 0)
+    spread_open(1, 1)
+    net.got("wsLB", "wsRA")
+    partial(2, 1)
+    middle(2, 0)
+    middle(2, 1)
+    spread_forward(1, 0)
+    spread_forward(1, 1)
+    finish(2, 0)
+    finish(2, 1)
+    along_x_take("w", w2, "OA")
+    along_x_take("w", w2, "OB")
+    partial(3, 0)
+    spread_open(2, 0)
+    spread_open(2, 1)
+    net.got("wsOA", "wsOB")
+    partial(3, 1)
+    along_x_take("p", pj, "LA")
+    along_x_take("p", pj, "RB")
+    along_x_open("t", tg)
+    middle(3, 0)
+    middle(3, 1)
+    spread_forward(2, 0)
+    spread_forward(2, 1)
+    finish(3, 0)
+    finish(3, 1)
+    net.got("psIA", "psIB")
+    predict(0)
+    spread_open(3, 0)
+    spread_open(3, 1)
+    net.got("psLA", "psRB")
+    predict(1)
+    along_x_take("p", pj, "LB")
+    along_x_take("p", pj, "RA")
+    spread_forward(3, 0)
+    spread_forward(3, 1)
+    net.got("psLB", "psRA")
+    predict(2)
+    along_x_take("p", pj, "OA")
+    along_x_take("p", pj, "OB")
+    along_x_take("t", tg, "LA")
+    along_x_take("t", tg, "RB")
+    net.got("tsIA", "tsIB")
+    subtract_target(landed(0))
+    net.got("psOA", "psOB")
+    predict(3)
+
+    h0 = lax.rem(t, 2)
+    d0 = lax.div(t, 2)
+    k0 = lax.rem(lax.div(d0, 2) - x + 4, 4)
+    k_odd, k_two = lax.rem(k0, 2), lax.div(k0, 2)
+    g0 = (1 - k_odd) * k_two * 3 + k_odd * (k_two * (1 + h0) + (1 - k_two) * (2 - h0))
+    i0 = (1 - k_odd) * h0 + k_odd * (1 - k_two)
+    pq0 = lax.rem(d0 + c, 2)
+    out[...] = so[g0, pq0, :, :, :, pl.ds(pl.multiple_of(i0 * 256, 256), 256)].reshape(512, 256)
+
+    net.got("tsLA", "tsRB")
+    subtract_target(landed(1))
+    along_x_take("t", tg, "LB")
+    along_x_take("t", tg, "RA")
+    net.got("tsLB", "tsRA")
+    subtract_target(landed(2))
+    along_x_take("t", tg, "OA")
+    along_x_take("t", tg, "OB")
+    net.got("tsOA", "tsOB")
+    subtract_target(landed(3))
+
+    loss_s[0] = row_squares(res[...])
+    stat_open("ly", loss_s.at[0], loss_y, "y", y)
+    loss_s[1] = stat_take("ly", loss_s.at[0], loss_y)
+    stat_open("lz", loss_s.at[1], loss_z, "z", z)
+    total = jnp.sum(stat_take("lz", loss_s.at[1], loss_z), axis=0, keepdims=True)
+    loss[...] = total / HT
+    net.drain()
+
+
+def call_second(hid, wd, pj, xrow, th, tgain, dest):
+    vm = pl.BlockSpec(memory_space=pltpu.VMEM)
+    hb = pl.BlockSpec(memory_space=pl.ANY)
+    return pl.pallas_call(
+        second_kernel,
+        name="second",
+        out_shape=(
+            jax.ShapeDtypeStruct((512, 256), BF),
+            jax.ShapeDtypeStruct((512, 512), F32),
+            jax.ShapeDtypeStruct((1, 512), F32),
+        ),
+        in_specs=[vm, hb, hb, vm, vm, vm, vm],
+        out_specs=(vm, vm, vm),
+        scratch_shapes=[
+            pltpu.VMEM((8, 2, 896, 256), BF),
+            pltpu.VMEM((8, 2, 256, 512), BF),
+            pltpu.VMEM((8, 2, 256, 512), BF),
+            pltpu.VMEM((4, 2, 4, 4, 32, 512), BF),
+            pltpu.VMEM((4, 2, 4, 4, 32, 512), BF),
+            pltpu.VMEM((4, 2, 3, 4, 32, 512), BF),
+            pltpu.VMEM((4, 2, 3, 32, 512), BF),
+            pltpu.VMEM((4, 2, 3, 32, 512), BF),
+            pltpu.VMEM((3, 8, 512), F32),
+            pltpu.VMEM((3, 8, 512), F32),
+            pltpu.VMEM((2, 8, 512), F32),
+            pltpu.VMEM((3, 8, 512), F32),
+            pltpu.VMEM((3, 8, 512), F32),
+            pltpu.VMEM((2, 8, 512), F32),
+            pltpu.SemaphoreType.DMA((4,)),
+            pltpu.SemaphoreType.DMA((N2,)),
+            pltpu.SemaphoreType.DMA((N2,)),
+        ],
+        compiler_params=pltpu.CompilerParams(
+            collective_id=1, has_side_effects=True, vmem_limit_bytes=67043328
+        ),
+    )(hid, wd, pj, xrow, th, tgain, dest)
 
 
 def local(
@@ -319,30 +647,13 @@
     w_down,
     proj,
 ):
-    t = lax.axis_index(TENSOR)
-    d = lax.axis_index(DP)
     hidden, th, xrow = call_first(
         attn_ctx, w_out, resid, student_in, student_gain.reshape(16, 256), w_gate, w_up
     )
-    ssq = lax.psum(jnp.sum(th * th, axis=1), TENSOR)
-    gain = lax.dynamic_slice_in_dim(teacher_gain, t * 512, 512, 0).astype(F32)
-    final = (th * lax.rsqrt(ssq / HT + 1e-06)[:, None] * gain[None, :]).astype(BF)
-    everyone = lax.all_gather(final, DP, axis=0, tiled=True)
-    pick = (dest_row[None, :] == (d * 512 + jnp.arange(512))[:, None]).astype(BF)
-    target = jnp.dot(pick, everyone, preferred_element_type=F32)
-    partial_sum = jnp.dot(
-        hidden, lax.all_gather(w_down, DP, axis=1, tiled=True), preferred_element_type=F32
+    out, residue, loss = call_second(
+        hidden, w_down, proj, xrow, th, teacher_gain.reshape(16, 1, 512), dest_row.reshape(16, 1, 256)
     )
-    rows = lax.psum_scatter(partial_sum.astype(BF), TENSOR, scatter_dimension=0, tiled=True).astype(F32)
-    out_rows = (rows + xrow.transpose(1, 0, 2).reshape(32, 4096).astype(F32)).astype(BF)
-    out_full = lax.all_gather(out_rows, TENSOR, axis=0, tiled=True)
-    out_local = lax.dynamic_slice_in_dim(out_full, t * 256, 256, 1)
-    pred = jnp.dot(
-        out_full, lax.all_gather(proj, DP, axis=0, tiled=True), preferred_element_type=F32
-    )
-    residue = pred - target
-    row_loss = one_axis_at_a_time(jnp.sum(residue * residue, axis=1), TENSOR) / HT
-    return (out_local, row_loss, residue)
+    return (out, loss.reshape(512), residue)
 
 
 def solution(mesh):

time: 361 us -> 207 us (0.57)
  waiting for transfers between devices: 150 us -> 0 us
  Pallas kernels: 107 us -> 198 us
  blocking collectives: 59.3 us -> 0 us
  matrix products: 20.6 us -> 0 us
  between operations: 13.9 us -> 0.65 us
  other arithmetic: 4.19 us -> 0 us
    pallas_call x0 -> x1, Pallas kernels: none -> 106 us  [call_second(): pl.pallas_call(second_kernel, name='second', out_shape=(jax.ShapeDtypeStr...]
    reduce_scatter x1 -> x0, waiting for transfers between devices: 76.2 us -> none  [local(): lax.psum_scatter(partial_sum.astype(BF), TENSOR, scatter_dimension=0, til...]
    all_gather x4 -> x0, waiting for transfers between devices: 73 us -> none  [the longest x1 45.1 us: local(): out_full = lax.all_gather(out_rows, TENSOR, axis=0, tiled=True)]
    psum x3 -> x0, blocking collectives: 59.3 us -> none  [the longest x1 38.1 us: local(): ssq = lax.psum(jnp.sum(th * th, axis=1), TENSOR)]
    dot_general x3 -> x0, matrix products: 20.6 us -> none  [the longest x1 9.98 us: local(): jnp.dot(hidden, lax.all_gather(w_down, DP, axis=1, tiled=True), preferred...]
    pallas_call x1, Pallas kernels: 107 us -> 92.5 us  [call_first(): pl.pallas_call(first_kernel, name='first', out_shape=(jax.ShapeDtypeStruc...]
    unnamed x7 -> x3, local copies, waits for them, and re-layouts: 1.45 us -> 5.18 us
  transfers between devices with their start and end apart: 5 -> 0, of which waited for: 3 -> 0; matrix products, arithmetic and copies ran while one was open for 3% -> 0% of each run, Pallas kernels for 30% -> 0%
where the time goes in v2:
time: 207 us
  Pallas kernels  198 us (96%)
  local copies, waits for them, and re-layouts  7.83 us (4%)
    pallas_call x1, Pallas kernels, call_second(): pl.pallas_call(second_kernel, name='second', out_shape=(jax.ShapeDtypeStr...  106 us
    pallas_call x1, Pallas kernels, call_first(): pl.pallas_call(first_kernel, name='first', out_shape=(jax.ShapeDtypeStruc...  92.5 us
    unnamed x3, local copies, waits for them, and re-layouts  5.18 us

profile of v2, /device:TPU:0, one launch (start us, length us, event | category | flops | bytes accessed | tf_op | source)
XLA Modules:
  0.0 206.7 jit_solution(16104861970680178177)
XLA Ops:
  0.6 1.3 reshape.18.gain
  1.9 1.3 reshape.22.tgain
  3.3 92.5 %first.1 = (bf16[512,896]{1,0:T(8,128)(2,1)}, f32[512,512]{1,0:T(8,128)}, bf16[16,32,256]{2,1,0:T(8,128)(2,1)}) custom-call(bf16[512,512]{1,0:T(8,128)(2,1)} %attn.1, bf16[512,8192]{1,0:T(8,128)(2,1)} %wout_hbm.1, bf16[32,8192]{1,0:T(8,128)(2,1)} %resid.1, bf16[512,256]{1,0:T(8,128)(2,1)} %sin.1, bf16[16,256]{1,0:T(8,128)(2,1)} %reshape.18.gain, ...), custom_call_target="tpu_custom_call" | custom-call | tf_op jit(solution)/shard_map/first/pallas_call | solution.py:268
  95.8 105.7 %second.1 = (bf16[512,256]{1,0:T(8,128)(2,1)}, f32[512,512]{1,0:T(8,128)}, f32[1,512]{1,0:T(1,128)}) custom-call(bf16[512,896]{1,0:T(8,128)(2,1)} %get-tuple-element.9.hid, bf16[896,512]{1,0:T(8,128)(2,1)} %wd_hbm.1, bf16[512,512]{1,0:T(8,128)(2,1)} %pj_hbm.1, bf16[16,32,256]{2,1,0:T(8,128)(2,1)} %get-tuple-element.10.xrow, ...), custom_call_target="tpu_custom_call" | custom-call | tf_op jit(solution)/shard_map/second/pallas_call | solution.py:602
  201.5 1.7 copy.18
  203.2 1.2 copy.19
  204.4 2.3 %copy.20 = f32[512,512]{1,0:T(8,128)} copy(f32[512,512]{1,0:T(8,128)} %get-tuple-element.20) | data formatting | bytes 2097152

commit v3 on v2

--- a/solution.py
+++ b/solution.py
@@ -48,7 +48,7 @@
     pl.semaphore_wait(barrier, len(partners))
 
 
-N1 = 68
+N1 = 92
 
 
 def first_kernel(
@@ -74,11 +74,19 @@
     loads.append(pltpu.make_async_copy(sin, xg.at[z, y], loc.at[4]))
     for cp in loads:
         cp.start()
-    wloads = [
-        pltpu.make_async_copy(wout_hbm.at[:, pl.ds(b * 512, 512)], wout.at[b], wsem.at[b]) for b in range(16)
-    ]
-    for cp in wloads:
-        cp.start()
+
+    order = (
+        (1, 1), (1, 2), (2, 1), (1, 3), (3, 1), (2, 2), (2, 3), (3, 2), (3, 3),
+        (0, 1), (1, 0), (0, 2), (2, 0), (0, 3), (3, 0), (0, 0),
+    )
+
+    def block_cols(dz, dy):
+        return pl.ds(pl.multiple_of((at(z, dz) * 4 + at(y, dy)) * 512, 512), 512)
+
+    wloads = {
+        b: pltpu.make_async_copy(wout_hbm.at[:, block_cols(*b)], wout.at[i], wsem.at[i])
+        for i, b in enumerate(order)
+    }
 
     greet(
         [sib, right, left]
@@ -90,12 +98,13 @@
     def piece(who, half):
         return pl.ds(who * 256 + half * 128, 128)
 
-    def ring_open(tag, axis, base, ref):
+    def ring_open(tag, axis, base, ref, src=None):
         up, down = {axis: at(base, 1)}, {axis: at(base, 3)}
-        net.send(tag + "LA", ref(0, 0), ref(0, 0), up)
-        net.send(tag + "RB", ref(0, 1), ref(0, 1), down)
-        net.send(tag + "LB", ref(0, 1), ref(0, 1), up)
-        net.send(tag + "RA", ref(0, 0), ref(0, 0), down)
+        src = src or (lambda h: ref(0, h))
+        net.send(tag + "LA", src(0), ref(0, 0), up)
+        net.send(tag + "RB", src(1), ref(0, 1), down)
+        net.send(tag + "LB", src(1), ref(0, 1), up)
+        net.send(tag + "RA", src(0), ref(0, 0), down)
 
     def ring_forward(tag, axis, base, ref):
         up, down = {axis: at(base, 1)}, {axis: at(base, 3)}
@@ -112,66 +121,94 @@
     p2 = lambda k, h: xg.at[at(z, k), :, piece(0, h)]
     q2 = lambda k, h: xg.at[:, at(y, k), piece(1, h)]
 
-    loads[4].wait()
-    ring_open("p1", "y", y, p1)
-    ring_open("q1", "z", z, q1)
+    ring_open("p1", "y", y, p1, lambda h: sin.at[piece(0, h)])
+    ring_open("q1", "z", z, q1, lambda h: sin.at[piece(1, h)])
     for cp in loads[:4]:
         cp.wait()
     net.send("wLA", w1.at[d, 0], w1.at[d, 0], right)
     net.send("wRB", w1.at[d, 1], w1.at[d, 1], left)
     net.send("wLB", w1.at[d, 1], w1.at[d, 1], right)
     net.send("wRA", w1.at[d, 0], w1.at[d, 0], left)
+    for b in order:
+        wloads[b].start()
     net.send("sIA", w1.at[d, 0], w1.at[d, 0], sib)
     net.send("sIB", w1.at[d, 1], w1.at[d, 1], sib)
 
     mine = pl.ds(pl.multiple_of(t * 32, 32), 32)
 
     def partial(b):
+        i = order.index(b)
         wloads[b].wait()
-        tmp[...] = jnp.dot(attn[...], wout[b], preferred_element_type=F32)
-        tmp[mine, :] += resid[:, b * 512:(b + 1) * 512].astype(F32)
-        part[b] = tmp[...].astype(BF)
-
-    partial(0)
-    partial(1)
-    partial(2)
-    partial(3)
+        tmp[...] = jnp.dot(attn[...], wout[i], preferred_element_type=F32)
+        tmp[mine, :] += resid[:, block_cols(*b)].astype(F32)
+        part[b[0] * 4 + b[1]] = tmp[...].astype(BF)
+
+    def term(pq, k, j, h):
+        b = k * 4 + j if pq == 0 else j * 4 + k
+        return b, pl.ds(pq * 256 + h * 128, 128)
+
+    def sum_dev(pq, j):
+        return {"y": at(y, j)} if pq == 0 else {"z": at(z, j)}
+
+    inbox = (rp, rq)
+
+    def sum_send(name, pq, k, j, h, slot, to):
+        b, rows = term(pq, k, j, h)
+        net.send(f"{name}{pq}{k}", part.at[b, rows], inbox[pq].at[k, slot], sum_dev(pq, to))
+
+    def sum_open(pq, k):
+        sum_send("fA", pq, k, 2, 0, 0, 1)
+        sum_send("fB", pq, k, 2, 1, 1, 3)
+        sum_send("uB", pq, k, 1, 1, 3, 1)
+        sum_send("dA", pq, k, 3, 0, 4, 3)
+
+    def sum_pass(pq, k):
+        for name, j, h, slot, out, to in (("fA", 1, 0, 0, "uA", 1), ("fB", 3, 1, 1, "dB", 3)):
+            net.got(f"{name}{pq}{k}")
+            b, rows = term(pq, k, j, h)
+            part[b, rows, :] = (part[b, rows, :].astype(F32) + inbox[pq][k, slot].astype(F32)).astype(BF)
+            sum_send(out, pq, k, j, h, 2 if out == "uA" else 5, to)
+
+    def sum_close(pq, k):
+        net.got(*[f"{name}{pq}{k}" for name in ("uA", "uB", "dA", "dB")])
+        store, box = (sp, rp2) if pq == 0 else (sq, rq2)
+        for h in range(2):
+            b, rows = term(pq, k, 0, h)
+            s = part[b, rows, :].astype(F32)
+            s = s + inbox[pq][k, 2 + h].astype(F32) + inbox[pq][k, 4 + h].astype(F32)
+            if k == 0:
+                th[rows, :] = s
+            else:
+                store[k - 1, h * 128:h * 128 + 128] = s.astype(BF)
+        if k:
+            dev = {"z": at(z, k)} if pq == 0 else {"y": at(y, k)}
+            net.send(f"v{pq}{k}", store.at[k - 1], box.at[k - 1], dev)
+
+    for b in order[:5]:
+        partial(b)
     ring_forward("p1", "y", y, p1)
     ring_forward("q1", "z", z, q1)
-    partial(4)
-    partial(5)
+    sum_open(0, 1)
+    sum_open(1, 1)
+    partial(order[5])
+    partial(order[6])
+    loads[4].wait()
     ring_close("p1")
     ring_open("p2", "z", z, p2)
     ring_close("q1")
     ring_open("q2", "y", y, q2)
-    for b in range(6, 16):
+    partial(order[7])
+    partial(order[8])
+    sum_pass(0, 1)
+    sum_pass(1, 1)
+    for b in order[9:]:
         partial(b)
+    sum_open(0, 2)
+    sum_open(1, 2)
     ring_forward("p2", "z", z, p2)
     ring_forward("q2", "y", y, q2)
-
-    P_ROWS, Q_ROWS = pl.ds(0, 256), pl.ds(256, 256)
-    for k in (1, 2, 3, 0):
-        for j in (1, 2, 3):
-            zz, yy = at(z, k), at(y, j)
-            net.send(f"tp{k}{j}", part.at[zz * 4 + yy, P_ROWS], rp.at[j - 1, k], {"y": yy})
-            zz, yy = at(z, j), at(y, k)
-            net.send(f"tq{k}{j}", part.at[zz * 4 + yy, Q_ROWS], rq.at[j - 1, k], {"z": zz})
-
-    ring_close("p2")
-    ring_close("q2")
-    xrow[...] = xg[:, :, mine, :].reshape(16, 32, 256)
-
-    @pl.loop(0, 4)
-    def _(r):
-        rows = pl.ds(pl.multiple_of(r * 128, 128), 128)
-        total = jnp.zeros((128, 256), F32)
-        for s in range(16):
-            v = xg[s // 4, s % 4, rows, :].astype(F32)
-            total = total + v * v
-        scale = lax.rsqrt(jnp.sum(total, axis=1, keepdims=True) / 4096.0 + 1e-05)
-        for s in range(16):
-            v = xg[s // 4, s % 4, rows, :].astype(F32)
-            nrm[s, rows, :] = (v * scale * gain[s:s + 1, :].astype(F32)).astype(BF)
+    sum_open(0, 3)
+    sum_open(1, 3)
 
     def gate_up(slots, first):
         @pl.loop(0, 7)
@@ -198,51 +235,53 @@
     net.got("wRB")
     net.send("wOB", w1.at[slot(xr, c), 1], w1.at[slot(xr, c), 1], left)
     pass_on("sRB", slot(xr, c), 1)
+    sum_pass(0, 2)
+    sum_pass(1, 2)
+    sum_open(0, 0)
+    sum_open(1, 0)
+
+    ring_close("p2")
+    ring_close("q2")
+    xrow[...] = xg[:, :, mine, :].reshape(16, 32, 256)
+
+    @pl.loop(0, 4)
+    def _(r):
+        rows = pl.ds(pl.multiple_of(r * 128, 128), 128)
+        total = jnp.zeros((128, 256), F32)
+        for s in range(16):
+            v = xg[s // 4, s % 4, rows, :].astype(F32)
+            total = total + v * v
+        scale = lax.rsqrt(jnp.sum(total, axis=1, keepdims=True) / 4096.0 + 1e-05)
+        for s in range(16):
+            v = xg[s // 4, s % 4, rows, :].astype(F32)
+            nrm[s, rows, :] = (v * scale * gain[s:s + 1, :].astype(F32)).astype(BF)
+
+    sum_pass(0, 3)
+    sum_pass(1, 3)
     net.got("sIA", "sIB")
     gate_up([(d, 0), (d, 1), (slot(x, 1 - c), 0), (slot(x, 1 - c), 1)], True)
+    sum_close(0, 1)
+    sum_close(1, 1)
+    sum_pass(0, 0)
+    sum_pass(1, 0)
     net.got("sLA", "sRB")
     gate_up([(slot(xl, c), 0), (slot(xr, c), 1), (slot(xl, 1 - c), 0), (slot(xr, 1 - c), 1)], False)
-
-    def reduce_p(k):
-        net.got(f"tp{k}1", f"tp{k}2", f"tp{k}3")
-        zz = at(z, k)
-        s = part[zz * 4 + y, :256, :].astype(F32)
-        for j in range(3):
-            s = s + rp[j, k].astype(F32)
-        if k == 0:
-            th[:256, :] = s
-        else:
-            sp[k - 1] = s.astype(BF)
-            net.send(f"up{k}", sp.at[k - 1], rp2.at[k - 1], {"z": zz})
-
-    def reduce_q(k):
-        net.got(f"tq{k}1", f"tq{k}2", f"tq{k}3")
-        yy = at(y, k)
-        s = part[z * 4 + yy, 256:, :].astype(F32)
-        for j in range(3):
-            s = s + rq[j, k].astype(F32)
-        if k == 0:
-            th[256:, :] = s
-        else:
-            sq[k - 1] = s.astype(BF)
-            net.send(f"uq{k}", sq.at[k - 1], rq2.at[k - 1], {"y": yy})
-
-    reduce_p(1)
-    reduce_q(1)
     net.got("wLB")
     pass_on("sLB", slot(xl, c), 1)
     net.got("wRA")
     pass_on("sRA", slot(xr, c), 0)
+    sum_close(0, 2)
+    sum_close(1, 2)
     net.got("sLB", "sRA")
     gate_up([(slot(xl, c), 1), (slot(xr, c), 0), (slot(xl, 1 - c), 1), (slot(xr, 1 - c), 0)], False)
-    reduce_p(2)
-    reduce_q(2)
+    sum_close(0, 3)
+    sum_close(1, 3)
     net.got("wOA")
     pass_on("sOA", slot(xo, c), 0)
     net.got("wOB")
     pass_on("sOB", slot(xo, c), 1)
-    reduce_p(3)
-    reduce_q(3)
+    sum_close(0, 0)
+    sum_close(1, 0)
     net.got("sOA", "sOB")
     gate_up([(slot(xo, c), 0), (slot(xo, c), 1), (slot(xo, 1 - c), 0), (slot(xo, 1 - c), 1)], False)
 
@@ -252,12 +291,10 @@
         u = acc[:, pl.ds(pl.multiple_of(896 + j * 128, 128), 128)]
         hid[:, pl.ds(pl.multiple_of(j * 128, 128), 128)] = (jax.nn.silu(g) * u).astype(BF)
 
-    reduce_p(0)
-    reduce_q(0)
     for k in (1, 2, 3):
-        net.got(f"up{k}")
+        net.got(f"v0{k}")
         th[:256, :] += rp2[k - 1].astype(F32)
-        net.got(f"uq{k}")
+        net.got(f"v1{k}")
         th[256:, :] += rq2[k - 1].astype(F32)
     net.drain()
 
@@ -281,8 +318,8 @@
             pltpu.VMEM((16, 512, 256), BF),
             pltpu.VMEM((16, 512, 512), BF),
             pltpu.VMEM((16, 512, 512), BF),
-            pltpu.VMEM((3, 4, 256, 512), BF),
-            pltpu.VMEM((3, 4, 256, 512), BF),
+            pltpu.VMEM((4, 6, 128, 512), BF),
+            pltpu.VMEM((4, 6, 128, 512), BF),
             pltpu.VMEM((3, 256, 512), BF),
             pltpu.VMEM((3, 256, 512), BF),
             pltpu.VMEM((3, 256, 512), BF),
@@ -300,13 +337,13 @@
     )(attn, wout, resid, sin, gain, wg, wu)
 
 
-N2 = 174
+N2 = 192
 
 
 def second_kernel(
     hid, wd_hbm, pj_hbm, xrow, th, tgain, dest,
     out, res, loss,
-    w2, pj, tg, pt, so, r1, s1, r2, stat_y, stat_z, stat_s, loss_y, loss_z, loss_s, loc, ss, rs,
+    w2, pj, tg, pt, so, r1, s1, r2, stat_in, stat_s, loss_in, loss_s, loc, ss, rs,
 ):
     x, c, z, y = (lax.axis_index(a) for a in AXES)
     t = z * 4 + y
@@ -326,8 +363,7 @@
         cp.start()
     greet(
         [sib, right, left]
-        + [{"y": at(y, k)} for k in (1, 2, 3)]
-        + [{"z": at(z, k)} for k in (1, 2, 3)]
+        + [{"z": at(z, i), "y": at(y, j)} for i in range(4) for j in range(4) if (i, j) != (0, 0)]
     )
     net = Net(ss, rs)
     owner = {"I": x, "L": xl, "R": xr, "O": xo}
@@ -455,13 +491,18 @@
             parts = parts + v[8 * i:8 * i + 8, :]
         return parts
 
-    def stat_open(tag, own, inbox, axis, base):
-        for j in (1, 2, 3):
-            net.send(f"{tag}{j}", own, inbox.at[j - 1], {axis: at(base, j)})
+    others = [(i, j) for i in range(4) for j in range(4) if (i, j) != (0, 0)]
+
+    def stat_open(tag, own, inbox):
+        for n, (i, j) in enumerate(others):
+            net.send(f"{tag}{n}", own, inbox.at[n], {"z": at(z, i), "y": at(y, j)})
 
     def stat_take(tag, own, inbox):
-        net.got(*[f"{tag}{j}" for j in (1, 2, 3)])
-        return own[...] + inbox[0] + inbox[1] + inbox[2]
+        net.got(*[f"{tag}{n}" for n in range(15)])
+        total = own[...]
+        for n in range(15):
+            total = total + inbox[n]
+        return jnp.sum(total, axis=0, keepdims=True)
 
     def landed(g):
         return target_of(groups[g], c) + target_of(groups[g], 1 - c)
@@ -480,92 +521,81 @@
             total = term if total is None else total + term
         res[...] -= total
 
-    stat_s[0] = row_squares(th[...])
-    stat_open("ty", stat_s.at[0], stat_y, "y", y)
+    def finish_target():
+        scale = lax.rsqrt(stat_take("q", stat_s, stat_in) / HT + 1e-06)
+        scale = jnp.broadcast_to(scale, (128, 512)).T
+        gain = tgain[t].astype(F32)
+        for h in range(2):
+            for i in range(4):
+                rows, cols = slice(h * 256, h * 256 + 256), slice(i * 128, i * 128 + 128)
+                tg[d, h, :, cols] = (th[rows, cols] * scale[rows, :] * gain[:, cols]).astype(BF)
+
+    def both(step, g):
+        step(g, 0)
+        step(g, 1)
+
+    def take_two(tag, buf, g):
+        along_x_take(tag, buf, groups[g][0])
+        along_x_take(tag, buf, groups[g][1])
+
+    def sibling_has(tag, g):
+        net.got(tag + "s" + groups[g][0], tag + "s" + groups[g][1])
+
+    def partials(g):
+        partial(g, 0)
+        sibling_has("w", g)
+        partial(g, 1)
+
     for cp in w2_loads:
         cp.wait()
     along_x_open("w", w2)
     partial(0, 0)
-    stat_s[1] = stat_take("ty", stat_s.at[0], stat_y)
-    stat_open("tz", stat_s.at[1], stat_z, "z", z)
-    net.got("wsIA", "wsIB")
+    stat_s[...] = row_squares(th[...])
+    stat_open("q", stat_s, stat_in)
+    sibling_has("w", 0)
     partial(0, 1)
-    total = jnp.sum(stat_take("tz", stat_s.at[1], stat_z), axis=0, keepdims=True)
-    scale = jnp.broadcast_to(lax.rsqrt(total / HT + 1e-06), (128, 512)).T
-    gain = tgain[t].astype(F32)
-    for h in range(2):
-        for i in range(4):
-            rows, cols = slice(h * 256, h * 256 + 256), slice(i * 128, i * 128 + 128)
-            tg[d, h, :, cols] = (th[rows, cols] * scale[rows, :] * gain[:, cols]).astype(BF)
-    middle(0, 0)
-    middle(0, 1)
-    finish(0, 0)
-    finish(0, 1)
-    along_x_take("w", w2, "LA")
-    along_x_take("w", w2, "RB")
-    partial(1, 0)
-    spread_open(0, 0)
-    spread_open(0, 1)
-    net.got("wsLA", "wsRB")
-    partial(1, 1)
+    both(middle, 0)
+    finish_target()
+    take_two("w", w2, 1)
+    partials(1)
     for cp in pj_loads:
         cp.wait()
     along_x_open("p", pj)
-    middle(1, 0)
-    middle(1, 1)
-    spread_forward(0, 0)
-    spread_forward(0, 1)
-    finish(1, 0)
-    finish(1, 1)
-    along_x_take("w", w2, "LB")
-    along_x_take("w", w2, "RA")
-    partial(2, 0)
-    spread_open(1, 0)
-    spread_open(1, 1)
-    net.got("wsLB", "wsRA")
-    partial(2, 1)
-    middle(2, 0)
-    middle(2, 1)
-    spread_forward(1, 0)
-    spread_forward(1, 1)
-    finish(2, 0)
-    finish(2, 1)
-    along_x_take("w", w2, "OA")
-    along_x_take("w", w2, "OB")
-    partial(3, 0)
-    spread_open(2, 0)
-    spread_open(2, 1)
-    net.got("wsOA", "wsOB")
-    partial(3, 1)
-    along_x_take("p", pj, "LA")
-    along_x_take("p", pj, "RB")
+    both(finish, 0)
+    both(spread_open, 0)
+    both(middle, 1)
+    take_two("w", w2, 2)
+    partials(2)
+    both(spread_forward, 0)
+    both(finish, 1)
+    both(spread_open, 1)
+    both(middle, 2)
+    take_two("w", w2, 3)
+    partials(3)
+    both(spread_forward, 1)
+    both(finish, 2)
+    take_two("p", pj, 1)
     along_x_open("t", tg)
-    middle(3, 0)
-    middle(3, 1)
-    spread_forward(2, 0)
-    spread_forward(2, 1)
-    finish(3, 0)
-    finish(3, 1)
-    net.got("psIA", "psIB")
+    both(spread_open, 2)
+    both(middle, 3)
+    sibling_has("p", 0)
     predict(0)
-    spread_open(3, 0)
-    spread_open(3, 1)
-    net.got("psLA", "psRB")
+    both(spread_forward, 2)
+    both(finish, 3)
+    take_two("p", pj, 2)
+    sibling_has("p", 1)
     predict(1)
-    along_x_take("p", pj, "LB")
-    along_x_take("p", pj, "RA")
-    spread_forward(3, 0)
-    spread_forward(3, 1)
-    net.got("psLB", "psRA")
+    both(spread_open, 3)
+    take_two("p", pj, 3)
+    sibling_has("p", 2)
     predict(2)
-    along_x_take("p", pj, "OA")
-    along_x_take("p", pj, "OB")
-    along_x_take("t", tg, "LA")
-    along_x_take("t", tg, "RB")
-    net.got("tsIA", "tsIB")
+    both(spread_forward, 3)
+    take_two("t", tg, 1)
+    sibling_has("t", 0)
     subtract_target(landed(0))
-    net.got("psOA", "psOB")
+    sibling_has("p", 3)
     predict(3)
+    take_two("t", tg, 2)
 
     h0 = lax.rem(t, 2)
     d0 = lax.div(t, 2)
@@ -576,23 +606,17 @@
     pq0 = lax.rem(d0 + c, 2)
     out[...] = so[g0, pq0, :, :, :, pl.ds(pl.multiple_of(i0 * 256, 256), 256)].reshape(512, 256)
 
-    net.got("tsLA", "tsRB")
+    sibling_has("t", 1)
     subtract_target(landed(1))
-    along_x_take("t", tg, "LB")
-    along_x_take("t", tg, "RA")
-    net.got("tsLB", "tsRA")
+    sibling_has("t", 2)
     subtract_target(landed(2))
-    along_x_take("t", tg, "OA")
-    along_x_take("t", tg, "OB")
-    net.got("tsOA", "tsOB")
+    take_two("t", tg, 3)
+    sibling_has("t", 3)
     subtract_target(landed(3))
 
-    loss_s[0] = row_squares(res[...])
-    stat_open("ly", loss_s.at[0], loss_y, "y", y)
-    loss_s[1] = stat_take("ly", loss_s.at[0], loss_y)
-    stat_open("lz", loss_s.at[1], loss_z, "z", z)
-    total = jnp.sum(stat_take("lz", loss_s.at[1], loss_z), axis=0, keepdims=True)
-    loss[...] = total / HT
+    loss_s[...] = row_squares(res[...])
+    stat_open("l", loss_s, loss_in)
+    loss[...] = stat_take("l", loss_s, loss_in) / HT
     net.drain()
 
 
@@ -618,12 +642,10 @@
             pltpu.VMEM((4, 2, 3, 4, 32, 512), BF),
             pltpu.VMEM((4, 2, 3, 32, 512), BF),
             pltpu.VMEM((4, 2, 3, 32, 512), BF),
-            pltpu.VMEM((3, 8, 512), F32),
-            pltpu.VMEM((3, 8, 512), F32),
-            pltpu.VMEM((2, 8, 512), F32),
-            pltpu.VMEM((3, 8, 512), F32),
-            pltpu.VMEM((3, 8, 512), F32),
-            pltpu.VMEM((2, 8, 512), F32),
+            pltpu.VMEM((15, 8, 512), F32),
+            pltpu.VMEM((8, 512), F32),
+            pltpu.VMEM((15, 8, 512), F32),
+            pltpu.VMEM((8, 512), F32),
             pltpu.SemaphoreType.DMA((4,)),
             pltpu.SemaphoreType.DMA((N2,)),
             pltpu.SemaphoreType.DMA((N2,)),

time: 207 us -> 188 us (0.908)
  Pallas kernels: 198 us -> 180 us
    pallas_call x1, Pallas kernels: 106 us -> 96 us  [call_second(): pl.pallas_call(second_kernel, name='second', out_shape=(jax.ShapeDtypeStr...]
    pallas_call x1, Pallas kernels: 92.5 us -> 83.7 us  [call_first(): pl.pallas_call(first_kernel, name='first', out_shape=(jax.ShapeDtypeStruc...]
where the time goes in v3:
time: 188 us
  Pallas kernels  180 us (96%)
  local copies, waits for them, and re-layouts  7.83 us (4%)
    pallas_call x1, Pallas kernels, call_second(): pl.pallas_call(second_kernel, name='second', out_shape=(jax.ShapeDtypeStr...  96 us
    pallas_call x1, Pallas kernels, call_first(): pl.pallas_call(first_kernel, name='first', out_shape=(jax.ShapeDtypeStruc...  83.7 us
    unnamed x3, local copies, waits for them, and re-layouts  5.18 us

profile of v3, /device:TPU:0, one launch (start us, length us, event | category | flops | bytes accessed | tf_op | source)
XLA Modules:
  0.0 188.1 jit_solution(11244435902272744306)
XLA Ops:
  0.6 1.3 reshape.18.gain
  1.9 1.3 reshape.22.tgain
  3.3 83.7 %first.1 = (bf16[512,896]{1,0:T(8,128)(2,1)}, f32[512,512]{1,0:T(8,128)}, bf16[16,32,256]{2,1,0:T(8,128)(2,1)}) custom-call(bf16[512,512]{1,0:T(8,128)(2,1)} %attn.1, bf16[512,8192]{1,0:T(8,128)(2,1)} %wout_hbm.1, bf16[32,8192]{1,0:T(8,128)(2,1)} %resid.1, bf16[512,256]{1,0:T(8,128)(2,1)} %sin.1, bf16[16,256]{1,0:T(8,128)(2,1)} %reshape.18.gain, ...), custom_call_target="tpu_custom_call" | custom-call | tf_op jit(solution)/shard_map/first/pallas_call | solution.py:305
  87.0 96.0 %second.1 = (bf16[512,256]{1,0:T(8,128)(2,1)}, f32[512,512]{1,0:T(8,128)}, f32[1,512]{1,0:T(1,128)}) custom-call(bf16[512,896]{1,0:T(8,128)(2,1)} %get-tuple-element.9.hid, bf16[896,512]{1,0:T(8,128)(2,1)} %wd_hbm.1, bf16[512,512]{1,0:T(8,128)(2,1)} %pj_hbm.1, bf16[16,32,256]{2,1,0:T(8,128)(2,1)} %get-tuple-element.10.xrow, ...), custom_call_target="tpu_custom_call" | custom-call | tf_op jit(solution)/shard_map/second/pallas_call | solution.py:626
  182.9 1.7 copy.18
  184.6 1.2 copy.19
  185.9 2.3 %copy.20 = f32[512,512]{1,0:T(8,128)} copy(f32[512,512]{1,0:T(8,128)} %get-tuple-element.20) | data formatting | bytes 2097152

commit v4 on v1

v4 whole, which is shorter than its diff:
```python
import jax
import jax.numpy as jnp
from jax import lax
from jax.sharding import Mesh
from jax.sharding import PartitionSpec as P
from jax.experimental import pallas as pl
from jax.experimental.pallas import tpu as pltpu

HT = 8192
BF = jnp.bfloat16
F32 = jnp.float32
AXES = ("x", "c", "z", "y")
TENSOR = ("z", "y")
DP = ("x", "c")
TRANSFERS = 284


class Net:
    def __init__(self, send_sems, recv_sems):
        self.ss, self.rs, self.made, self.left = send_sems, recv_sems, {}, set()

    def send(self, role, src, dst, dev):
        i = len(self.made)
        cp = pltpu.make_async_remote_copy(
            src_ref=src,
            dst_ref=dst,
            send_sem=self.ss.at[i],
            recv_sem=self.rs.at[i],
            device_id=dev,
            device_id_type=pl.DeviceIdType.MESH,
        )
        cp.start()
        self.made[role] = cp
        self.left.add(role)

    def got(self, *roles):
        for role in roles:
            self.made[role].wait_recv()

    def flush(self, *roles):
        for role in roles:
            self.made[role].wait_send()
            self.left.remove(role)

    def drain(self):
        self.flush(*[role for role in self.made if role in self.left])


def greet(partners):
    barrier = pltpu.get_barrier_semaphore()
    for dev in partners:
        pl.semaphore_signal(barrier, inc=1, device_id=dev, device_id_type=pl.DeviceIdType.MESH)
    pl.semaphore_wait(barrier, len(partners))


def kernel(
    attn, wout_hbm, resid, sin, gain, wg_hbm, wu_hbm, wd_hbm, pj_hbm, tgain, dest,
    out, res, loss,
    w1, xg, wout, part, rp, rq, sp, sq, rp2, rq2, acc, hid, xrow, w2, pj, r1, r2,
    stat_in, stat_s, loss_in, loss_s, loc, wsem, plane, ss, rs,
):
    x, c, z, y = (lax.axis_index(a) for a in AXES)
    t = z * 4 + y
    d = x * 2 + c

    def at(base, k):
        return lax.rem(base + k, 4)

    xr, xl, xo = at(x, 1), at(x, 3), at(x, 2)
    sib = {"c": 1 - c}
    right, left = {"x": xr}, {"x": xl}
    loads, w2_loads, pj_loads = [], [], []
    for h in range(2):
        rows = pl.ds(h * 256, 256)
        loads.append(pltpu.make_async_copy(wg_hbm.at[rows], w1.at[d, h, :, pl.ds(0, 896)], loc.at[2 * h]))
        loads.append(pltpu.make_async_copy(wu_hbm.at[rows], w1.at[d, h, :, pl.ds(896, 896)], loc.at[2 * h + 1]))
        w2_loads.append(pltpu.make_async_copy(wd_hbm.at[:, rows], w2.at[d, h], loc.at[5 + h]))
        pj_loads.append(pltpu.make_async_copy(pj_hbm.at[rows], pj.at[d, h], loc.at[7 + h]))
    loads.append(pltpu.make_async_copy(sin, xg.at[z, y], loc.at[4]))
    for cp in loads:
        cp.start()

    order = (
        (1, 1), (1, 2), (2, 1), (1, 3), (3, 1), (2, 2), (2, 3), (3, 2), (3, 3),
        (0, 1), (1, 0), (0, 2), (2, 0), (0, 3), (3, 0), (0, 0),
    )
    SLOTS = 4

    def block_cols(dz, dy):
        return pl.ds(pl.multiple_of((at(z, dz) * 4 + at(y, dy)) * 512, 512), 512)

    wloads = [
        pltpu.make_async_copy(wout_hbm.at[:, block_cols(*b)], wout.at[i % SLOTS], wsem.at[i % SLOTS])
        for i, b in enumerate(order)
    ]

    others = [(i, j) for i in range(4) for j in range(4) if (i, j) != (0, 0)]
    greet([sib, right, left] + [{a: at(b, k)} for a, b in (("y", y), ("z", z)) for k in (1, 2, 3)])
    net = Net(ss, rs)
    for k in (1, 2, 3):
        pl.semaphore_signal(plane, inc=1, device_id={"y": at(y, k)}, device_id_type=pl.DeviceIdType.MESH)

    def ring_open(tag, axis, base, ref, src=None):
        up, down = {axis: at(base, 1)}, {axis: at(base, 3)}
        src = src or (lambda h: ref(0, h))
        net.send(tag + "LA", src(0), ref(0, 0), up)
        net.send(tag + "RB", src(1), ref(0, 1), down)
        net.send(tag + "LB", src(1), ref(0, 1), up)
        net.send(tag + "RA", src(0), ref(0, 0), down)

    def ring_forward(tag, axis, base, ref):
        net.got(tag + "LA")
        net.send(tag + "OA", ref(3, 0), ref(3, 0), {axis: at(base, 1)})
        net.got(tag + "RB")
        net.send(tag + "OB", ref(1, 1), ref(1, 1), {axis: at(base, 3)})

    RING = ("LA", "RB", "LB", "RA", "OA", "OB")

    def ring_close(tag):
        net.got(*[tag + role for role in RING[2:]])

    p1 = lambda k, h: xg.at[z, at(y, k), h]
    q1 = lambda k, h: xg.at[at(z, k), y, 2 + h]
    p2 = lambda k, h: xg.at[at(z, k), :, h]
    q2 = lambda k, h: xg.at[:, at(y, k), 2 + h]

    owner = {"I": x, "L": xl, "R": xr, "O": xo}
    half = {"A": 0, "B": 1}
    groups = (("IA", "IB"), ("LA", "RB"), ("LB", "RA"), ("OA", "OB"))

    def shard(role, core):
        return owner[role[0]] * 2 + core, half[role[1]]

    w1_ref = lambda role, core: w1.at[shard(role, core)]
    w2_ref = lambda role, core: w2.at[shard(role, core)]
    pj_ref = lambda role, core: pj.at[shard(role, core)]

    def tg_ref(role, core):
        dd, h = shard(role, core)
        return w1.at[dd, h, :, pl.ds(0, 512)]

    def along_x_open(tag, ref):
        for role, own, dev in (("LA", "IA", right), ("RB", "IB", left), ("LB", "IB", right), ("RA", "IA", left)):
            net.send(tag + role, ref(own, c), ref(own, c), dev)
        for own in groups[0]:
            net.send(tag + "s" + own, ref(own, c), ref(own, c), sib)

    def along_x_take(tag, ref, g):
        for role in groups[g]:
            net.got(tag + role)
            block = ref(role, c)
            if role == "LA":
                net.send(tag + "OA", block, block, right)
            if role == "RB":
                net.send(tag + "OB", block, block, left)
            net.send(tag + "s" + role, block, block, sib)

    def sibling_has(tag, g):
        net.got(*[tag + "s" + role for role in groups[g]])

    def partial(i):
        b = order[i]
        wloads[i].wait()
        acc[:, :512] = jnp.dot(attn[...], wout[i % SLOTS], preferred_element_type=F32)
        if i + SLOTS < 16:
            wloads[i + SLOTS].start()
        rows = pl.ds(pl.multiple_of(t * 32, 32), 32)
        acc[rows, :512] += resid[:, block_cols(*b)].astype(F32)
        part[b[0] * 4 + b[1]] = acc[:, :512].astype(BF).reshape(4, 4, 32, 512)

    inbox = (rp, rq)

    def term(pq, k, j, h):
        return (k * 4 + j if pq == 0 else j * 4 + k), pq * 2 + h

    def sum_send(name, pq, k, j, h, slot, to):
        dev = {"y": at(y, to)} if pq == 0 else {"z": at(z, to)}
        net.send(f"{name}{pq}{k}", part.at[term(pq, k, j, h)], inbox[pq].at[k, slot], dev)

    def sum_open(k):
        for pq in range(2):
            sum_send("fA", pq, k, 2, 0, 0, 1)
            sum_send("fB", pq, k, 2, 1, 1, 3)
            sum_send("uB", pq, k, 1, 1, 3, 1)
            sum_send("dA", pq, k, 3, 0, 4, 3)

    def sum_pass(k):
        for pq in range(2):
            for name, j, h, slot, to_slot, send_as, to in (("fA", 1, 0, 0, 2, "uA", 1), ("fB", 3, 1, 1, 5, "dB", 3)):
                net.got(f"{name}{pq}{k}")
                b, rows = term(pq, k, j, h)
                part[b, rows] = (part[b, rows].astype(F32) + inbox[pq][k, slot].astype(F32)).astype(BF)
                sum_send(send_as, pq, k, j, h, to_slot, to)

    SUMS = ("fA", "fB", "uB", "dA", "uA", "dB")

    def sum_close(k):
        for pq in range(2):
            net.got(*[f"{name}{pq}{k}" for name in ("uA", "uB", "dA", "dB")])
            store, box = (sp, rp2) if pq == 0 else (sq, rq2)
            for h in range(2):
                b, rows = term(pq, k, 0, h)
                s = part[b, rows].astype(F32)
                s = s + inbox[pq][k, 2 + h].astype(F32) + inbox[pq][k, 4 + h].astype(F32)
                if k == 0:
                    res[pq * 256 + h * 128:pq * 256 + h * 128 + 128, :] = s.reshape(128, 512)
                else:
                    store[k - 1, h] = s.astype(BF)
            if k:
                dev = {"z": at(z, k)} if pq == 0 else {"y": at(y, k)}
                net.send(f"v{pq}{k}", store.at[k - 1], box.at[k - 1], dev)

    def teacher_hidden():
        for k in (1, 2, 3):
            net.got(f"v0{k}", f"v1{k}")
        for pq, box in ((0, rp2), (1, rq2)):
            rows = slice(pq * 256, pq * 256 + 256)
            s = box[0].astype(F32) + box[1].astype(F32) + box[2].astype(F32)
            res[rows, :] += s.reshape(256, 512)

    def slot_of(role, core):
        return xg.at[owner[role[0]], 2 * core + half[role[1]]]

    def gate_up(g):
        @pl.loop(0, 7)
        def _(j):
            cols = pl.ds(pl.multiple_of(j * 256, 256), 256)
            total = None
            for core in (c, 1 - c):
                for role in groups[g]:
                    dd, h = shard(role, core)
                    lhs = slot_of(role, core)[...].reshape(512, 256)
                    term = jnp.dot(lhs, w1[dd, h, :, cols], preferred_element_type=F32)
                    total = term if total is None else total + term
            if g == 0:
                acc[:, cols] = total
            else:
                acc[:, cols] += total

    free_blocks = ((5, 6), (7, 9), (10, 11), (13, 14))

    def down(g, pq):
        core = c if pq == 0 else 1 - c
        b = free_blocks[g][pq]
        for i in range(2):
            dd, h = shard(groups[g][i], core)
            piece = jnp.dot(hid[...], w2[dd, h], preferred_element_type=F32)
            part[b, :, :, :, i * 256:(i + 1) * 256] = piece.astype(BF).reshape(4, 4, 32, 256)
        for j in (1, 2, 3):
            if pq == 0:
                yy = at(y, j)
                net.send(f"a{g}0{j}", part.at[b, :, yy], r1.at[g, 0, j - 1], {"y": yy})
            else:
                zz = at(z, j)
                net.send(f"a{g}1{j}", part.at[b, zz], r1.at[g, 1, j - 1], {"z": zz})

    own_sum = {}

    def middle(g, pq):
        net.got(*[f"a{g}{pq}{j}" for j in (1, 2, 3)])
        b = free_blocks[g][pq]
        for k in (1, 2, 3, 0):
            other = at(z if pq == 0 else y, k)
            mine = part[b, other, y] if pq == 0 else part[b, z, other]
            s = mine.astype(F32)
            for j in range(3):
                s = s + r1[g, pq, j, other].astype(F32)
            if k == 0:
                own_sum[g, pq] = s
            else:
                n = (2 * g + pq) * 3 + k - 1
                where = (n // 8, n // 4 % 2, n % 4)
                sp[where] = s.astype(BF)
                dev = {"z": other} if pq == 0 else {"y": other}
                net.send(f"b{g}{pq}{k}", sp.at[where], r2.at[g, pq, k - 1], dev)

    def finish(g, pq):
        net.got(*[f"b{g}{pq}{j}" for j in (1, 2, 3)])
        s = own_sum[g, pq]
        for j in range(3):
            s = s + r2[g, pq, j].astype(F32)
        core = c if pq == 0 else 1 - c
        for i in range(2):
            dd, h = shard(groups[g][i], core)
            xin = xrow[dd * 2 + h].astype(F32)
            xg[g, 2 * pq + i, z, y] = (xin + s[:, i * 256:(i + 1) * 256]).astype(BF)
        ref = xg.at[g, pl.ds(2 * pq, 2), z, y]
        for j in (1, 2, 3):
            dev = {"y": at(y, j)} if pq == 0 else {"z": at(z, j)}
            net.send(f"c{g}{pq}{j}", ref, ref, dev)

    def spread_ring(g, pq):
        pair = pl.ds(2 * pq, 2)
        if pq == 0:
            return f"d{g}0", "z", z, lambda k, h: xg.at[g, pair, at(z, k), pl.ds(2 * h, 2)]
        return f"d{g}1", "y", y, lambda k, h: xg.at[g, pair, pl.ds(2 * h, 2), at(y, k)]

    def spread_open(g, pq):
        net.got(*[f"c{g}{pq}{j}" for j in (1, 2, 3)])
        ring_open(*spread_ring(g, pq))

    def spread_forward(g, pq):
        ring_forward(*spread_ring(g, pq))

    def predict(g):
        ring_close(f"d{g}0")
        ring_close(f"d{g}1")
        total = None
        for pq in range(2):
            core = c if pq == 0 else 1 - c
            for i in range(2):
                dd, h = shard(groups[g][i], core)
                lhs = xg[g, 2 * pq + i].reshape(512, 256)
                piece = jnp.dot(lhs, pj[dd, h], preferred_element_type=F32)
                total = piece if total is None else total + piece
        if g == 0:
            res[...] = total
        else:
            res[...] += total

    def row_squares(value):
        v = value * value
        v = v[:, 0:128] + v[:, 128:256] + v[:, 256:384] + v[:, 384:512]
        v = v.T
        parts = v[0:8, :]
        for i in range(1, 16):
            parts = parts + v[8 * i:8 * i + 8, :]
        return parts

    def stat_open(tag, own, box):
        for n, (i, j) in enumerate(others):
            net.send(f"{tag}{n}", own, box.at[n], {"z": at(z, i), "y": at(y, j)})

    def stat_take(tag, own, box):
        net.got(*[f"{tag}{n}" for n in range(15)])
        total = own[...]
        for n in range(15):
            total = total + box[n]
        return jnp.sum(total, axis=0, keepdims=True)

    def finish_target():
        scale = lax.rsqrt(stat_take("q", stat_s, stat_in) / HT + 1e-06)
        scale = jnp.broadcast_to(scale, (128, 512)).T
        eight = tgain[pl.ds(pl.multiple_of(lax.div(t, 2) * 8, 8), 8), :].astype(F32)
        four = jnp.where(lax.rem(t, 2) == 0, eight[0:4, :], eight[4:8, :])
        for h in range(2):
            for i in range(4):
                rows, cols = slice(h * 256, h * 256 + 256), slice(i * 128, i * 128 + 128)
                w1[d, h, :, cols] = (res[rows, cols] * scale[rows, :] * four[i:i + 1, :]).astype(BF)

    row_id = d * 512 + lax.broadcasted_iota(jnp.int32, (512, 256), 0)

    def subtract_target(g):
        total = None
        for core in (c, 1 - c):
            for role in groups[g]:
                dd, h = shard(role, core)
                onehot = jnp.where(row_id == dest[dd * 2 + h], 1.0, 0.0).astype(BF)
                piece = jnp.dot(onehot, w1[dd, h, :, 0:512], preferred_element_type=F32)
                total = piece if total is None else total + piece
        res[...] -= total

    def both(step, g):
        step(g, 0)
        step(g, 1)

    def downs(g):
        down(g, 0)
        sibling_has("m", g)
        down(g, 1)

    ring_open("p1", "y", y, p1, lambda h: sin.at[h])
    ring_open("q1", "z", z, q1, lambda h: sin.at[2 + h])
    for cp in loads[:4]:
        cp.wait()
    along_x_open("w", w1_ref)
    for i in range(SLOTS):
        wloads[i].start()
    for cp in w2_loads + pj_loads:
        cp.start()
    for i in range(5):
        partial(i)
    ring_forward("p1", "y", y, p1)
    ring_forward("q1", "z", z, q1)
    sum_open(1)
    partial(5)
    partial(6)
    loads[4].wait()
    ring_close("p1")
    ring_open("p2", "z", z, p2)
    ring_close("q1")
    ring_open("q2", "y", y, q2)
    partial(7)
    partial(8)
    sum_pass(1)
    for i in range(9, 16):
        partial(i)
    sum_open(2)
    ring_forward("p2", "z", z, p2)
    ring_forward("q2", "y", y, q2)
    sum_open(3)
    along_x_take("w", w1_ref, 1)
    for cp in w2_loads:
        cp.wait()
    along_x_open("m", w2_ref)
    sum_pass(2)
    sum_open(0)
    ring_close("p2")
    ring_close("q2")
    for tag in ("p1", "q1", "p2", "q2"):
        net.flush(*[tag + role for role in RING])
    xrow[...] = xg[:, :, z, y].reshape(16, 32, 256)

    @pl.loop(0, 4)
    def _(r):
        total = jnp.zeros((128, 256), F32)
        for s in range(16):
            v = xg[s // 4, s % 4, r].reshape(128, 256).astype(F32)
            total = total + v * v
        scale = lax.rsqrt(jnp.sum(total, axis=1, keepdims=True) / 4096.0 + 1e-05)
        for s in range(16):
            v = xg[s // 4, s % 4, r].reshape(128, 256).astype(F32)
            g = jnp.concatenate([gain[2 * s:2 * s + 1, :], gain[2 * s + 1:2 * s + 2, :]], axis=1)
            xg[s // 4, s % 4, r] = (v * scale * g.astype(F32)).astype(BF).reshape(4, 32, 256)

    sum_pass(3)
    sibling_has("w", 0)
    gate_up(0)
    sum_close(1)
    sibling_has("w", 1)
    gate_up(1)
    along_x_take("w", w1_ref, 2)
    sum_pass(0)
    sum_close(2)
    sibling_has("w", 2)
    gate_up(2)
    sum_close(3)
    along_x_take("w", w1_ref, 3)
    sibling_has("w", 3)
    gate_up(3)

    @pl.loop(0, 7)
    def _(j):
        g = acc[:, pl.ds(pl.multiple_of(j * 128, 128), 128)]
        u = acc[:, pl.ds(pl.multiple_of(896 + j * 128, 128), 128)]
        hid[:, pl.ds(pl.multiple_of(j * 128, 128), 128)] = (jax.nn.silu(g) * u).astype(BF)

    net.flush(*[f"{name}{pq}{k}" for name in SUMS for pq in range(2) for k in (1, 2, 3)])
    net.flush(*[f"v0{k}" for k in (1, 2, 3)])
    downs(0)
    net.flush(*["w" + s + role for g in groups for role in g for s in ("", "s") if s or role[0] != "I"])
    for cp in pj_loads:
        cp.wait()
    sum_close(0)
    along_x_take("m", w2_ref, 1)
    along_x_open("p", pj_ref)
    downs(1)
    both(middle, 0)
    teacher_hidden()
    stat_s[...] = row_squares(res[...])
    pl.semaphore_wait(plane, 3)
    stat_open("q", stat_s, stat_in)
    both(middle, 1)
    both(finish, 0)
    along_x_take("m", w2_ref, 2)
    downs(2)
    both(finish, 1)
    both(spread_open, 0)
    finish_target()
    both(middle, 2)
    along_x_take("m", w2_ref, 3)
    downs(3)
    both(spread_open, 1)
    both(spread_forward, 0)
    both(finish, 2)
    along_x_take("p", pj_ref, 1)
    sibling_has("p", 0)
    along_x_open("t", tg_ref)
    both(middle, 3)
    along_x_take("p", pj_ref, 2)
    both(spread_forward, 1)
    both(spread_open, 2)
    predict(0)
    both(finish, 3)
    along_x_take("p", pj_ref, 3)
    both(spread_forward, 2)
    sibling_has("p", 1)
    predict(1)
    both(spread_open, 3)
    along_x_take("t", tg_ref, 1)
    both(spread_forward, 3)
    sibling_has("p", 2)
    predict(2)
    sibling_has("t", 0)
    subtract_target(0)
    along_x_take("t", tg_ref, 2)
    sibling_has("p", 3)
    predict(3)

    h0 = lax.rem(t, 2)
    d0 = lax.div(t, 2)
    k0 = lax.rem(lax.div(d0, 2) - x + 4, 4)
    k_odd, k_two = lax.rem(k0, 2), lax.div(k0, 2)
    g0 = (1 - k_odd) * k_two * 3 + k_odd * (k_two * (1 + h0) + (1 - k_two) * (2 - h0))
    i0 = (1 - k_odd) * h0 + k_odd * (1 - k_two)
    out[...] = xg[g0, 2 * lax.rem(d0 + c, 2) + i0].reshape(512, 256)

    sibling_has("t", 1)
    subtract_target(1)
    sibling_has("t", 2)
    subtract_target(2)
    along_x_take("t", tg_ref, 3)
    sibling_has("t", 3)
    subtract_target(3)
    loss_s[...] = row_squares(res[...])
    stat_open("l", loss_s, loss_in)
    loss[...] = stat_take("l", loss_s, loss_in) / HT
    net.drain()


def call_kernel(*args):
    vm = pl.BlockSpec(memory_space=pltpu.VMEM)
    hb = pl.BlockSpec(memory_space=pl.ANY)
    return pl.pallas_call(
        kernel,
        name="first",
        out_shape=(
            jax.ShapeDtypeStruct((512, 256), BF),
            jax.ShapeDtypeStruct((512, 512), F32),
            jax.ShapeDtypeStruct((1, 512), F32),
        ),
        in_specs=[vm, hb, vm, vm, vm, hb, hb, hb, hb, vm, vm],
        out_specs=(vm, vm, vm),
        scratch_shapes=[
            pltpu.VMEM((8, 2, 256, 1792), BF),
            pltpu.VMEM((4, 4, 4, 4, 32, 256), BF),
            pltpu.VMEM((4, 512, 512), BF),
            pltpu.VMEM((16, 4, 4, 32, 512), BF),
            pltpu.VMEM((4, 6, 4, 32, 512), BF),
            pltpu.VMEM((4, 6, 4, 32, 512), BF),
            pltpu.VMEM((3, 2, 4, 32, 512), BF),
            pltpu.VMEM((3, 2, 4, 32, 512), BF),
            pltpu.VMEM((3, 2, 4, 32, 512), BF),
            pltpu.VMEM((3, 2, 4, 32, 512), BF),
            pltpu.VMEM((512, 1792), F32),
            pltpu.VMEM((512, 896), BF),
            pltpu.VMEM((16, 32, 256), BF),
            pltpu.VMEM((8, 2, 896, 256), BF),
            pltpu.VMEM((8, 2, 256, 512), BF),
            pltpu.VMEM((4, 2, 3, 4, 32, 512), BF),
            pltpu.VMEM((4, 2, 3, 32, 512), BF),
            pltpu.VMEM((15, 8, 512), F32),
            pltpu.VMEM((8, 512), F32),
            pltpu.VMEM((15, 8, 512), F32),
            pltpu.VMEM((8, 512), F32),
            pltpu.SemaphoreType.DMA((9,)),
            pltpu.SemaphoreType.DMA((4,)),
            pltpu.SemaphoreType.REGULAR,
            pltpu.SemaphoreType.DMA((TRANSFERS,)),
            pltpu.SemaphoreType.DMA((TRANSFERS,)),
        ],
        compiler_params=pltpu.CompilerParams(
            collective_id=0, has_side_effects=True, vmem_limit_bytes=67043328
        ),
    )(*args)


def keep(out, res, loss, out_to, res_to, loss_to):
    out_to[...] = out[...]
    res_to[...] = res[...]
    loss_to[...] = loss[...]


def local(
    attn_ctx,
    w_out,
    resid,
    teacher_gain,
    dest_row,
    student_in,
    student_gain,
    w_gate,
    w_up,
    w_down,
    proj,
):
    made = call_kernel(
        attn_ctx,
        w_out,
        resid,
        student_in.reshape(4, 4, 32, 256),
        student_gain.reshape(32, 128),
        w_gate,
        w_up,
        w_down,
        proj,
        teacher_gain.reshape(64, 128),
        dest_row.reshape(16, 1, 256),
    )
    vm = pl.BlockSpec(memory_space=pltpu.VMEM)
    out, residue, loss = pl.pallas_call(
        keep,
        name="keep",
        out_shape=tuple(jax.ShapeDtypeStruct(a.shape, a.dtype) for a in made),
        in_specs=[vm, vm, vm],
        out_specs=(vm, vm, vm),
    )(*made)
    return (out, loss.reshape(512), residue)


def solution(mesh):
    torus = Mesh(mesh.devices.reshape(4, 2, 4, 4), AXES)
    in_specs = (
        P(DP, TENSOR),
        P(TENSOR, None),
        P(DP + TENSOR, None),
        P(),
        P(),
        P(DP, TENSOR),
        P(),
        P(DP, TENSOR),
        P(DP, TENSOR),
        P(TENSOR, DP),
        P(DP, TENSOR),
    )
    out_specs = (P(DP, TENSOR), P(DP), P(DP, TENSOR))
    return jax.shard_map(local, mesh=torus, in_specs=in_specs, out_specs=out_specs, check_vma=False)
```

time: 361 us -> 158 us (0.44)
  waiting for transfers between devices: 150 us -> 0 us
  blocking collectives: 59.3 us -> 0 us
  Pallas kernels: 107 us -> 157 us
  matrix products: 20.6 us -> 0 us
  between operations: 13.9 us -> 0.64 us
  local copies, waits for them, and re-layouts: 4.46 us -> 0 us
  other arithmetic: 4.19 us -> 0 us
    reduce_scatter x1 -> x0, waiting for transfers between devices: 76.2 us -> none  [local(): lax.psum_scatter(partial_sum.astype(BF), TENSOR, scatter_dimension=0, til...]
    all_gather x4 -> x0, waiting for transfers between devices: 73 us -> none  [the longest x1 45.1 us: local(): out_full = lax.all_gather(out_rows, TENSOR, axis=0, tiled=True)]
    psum x3 -> x0, blocking collectives: 59.3 us -> none  [the longest x1 38.1 us: local(): ssq = lax.psum(jnp.sum(th * th, axis=1), TENSOR)]
    pallas_call x1 -> x2, Pallas kernels: 107 us -> 157 us  [the longest x1 154 us: call_kernel(): pl.pallas_call(kernel, name='first', out_shape=(jax.ShapeDtypeStruct((512...]
    dot_general x3 -> x0, matrix products: 20.6 us -> none  [the longest x1 9.98 us: local(): jnp.dot(hidden, lax.all_gather(w_down, DP, axis=1, tiled=True), preferred...]
  transfers between devices with their start and end apart: 5 -> 0, of which waited for: 3 -> 0; matrix products, arithmetic and copies ran while one was open for 3% -> 0% of each run, Pallas kernels for 30% -> 0%
where the time goes in v4:
time: 158 us; the launch traced here: 157 us
  Pallas kernels  157 us (99%)
    pallas_call x1, Pallas kernels, call_kernel(): pl.pallas_call(kernel, name='first', out_shape=(jax.ShapeDtypeStruct((512...  154 us

profile of v4, /device:TPU:0, one launch (start us, length us, event | category | flops | bytes accessed | tf_op | source)
XLA Modules:
  0.0 157.3 jit_solution(17175941195557237891)
XLA Ops:
  0.6 154.3 %first.1 = (bf16[512,256]{1,0:T(8,128)(2,1)}, f32[512,512]{1,0:T(8,128)}, f32[1,512]{1,0:T(1,128)}) custom-call(bf16[512,512]{1,0:T(8,128)(2,1)} %attn.1, bf16[512,8192]{1,0:T(8,128)(2,1)} %wout_hbm.1, bf16[32,8192]{1,0:T(8,128)(2,1)} %resid.1, bf16[4,4,32,256]{3,2,1,0:T(8,128)(2,1)} %bitcast.5, bf16[32,128]{1,0:T(8,128)(2,1)} %bitcast.8, ...), custom_call_target="tpu_custom_call" | custom-call | tf_op jit(solution)/shard_map/first/pallas_call | solution.py:524
  155.0 2.4 %keep.1 = (bf16[512,256]{1,0:T(8,128)(2,1)}, f32[512,512]{1,0:T(8,128)}, f32[1,512]{1,0:T(1,128)}) custom-call(bf16[512,256]{1,0:T(8,128)(2,1)} %get-tuple-element.9.out, f32[512,512]{1,0:T(8,128)} %get-tuple-element.10.res, f32[1,512]{1,0:T(1,128)} %get-tuple-element.11.loss), custom_call_target="tpu_custom_call" | custom-call | tf_op jit(solution)/shard_map/keep/pallas_call | solution.py:601

commit v5 on v4

--- a/solution.py
+++ b/solution.py
@@ -12,38 +12,35 @@
 AXES = ("x", "c", "z", "y")
 TENSOR = ("z", "y")
 DP = ("x", "c")
-TRANSFERS = 284
+SENDS, RECEIVES = 16, 113
 
 
 class Net:
     def __init__(self, send_sems, recv_sems):
-        self.ss, self.rs, self.made, self.left = send_sems, recv_sems, {}, set()
-
-    def send(self, role, src, dst, dev):
-        i = len(self.made)
+        self.ss, self.rs, self.sent, self.due, self.made = send_sems, recv_sems, {}, {}, {}
+
+    def send(self, out, role, src, dst, dev):
+        i = self.sent.setdefault(out, len(self.sent))
+        j = self.due.setdefault(role, len(self.due))
         cp = pltpu.make_async_remote_copy(
             src_ref=src,
             dst_ref=dst,
             send_sem=self.ss.at[i],
-            recv_sem=self.rs.at[i],
+            recv_sem=self.rs.at[j],
             device_id=dev,
             device_id_type=pl.DeviceIdType.MESH,
         )
         cp.start()
         self.made[role] = cp
-        self.left.add(role)
-
-    def got(self, *roles):
-        for role in roles:
+
+    def got(self, role, bytes_of=None):
+        if bytes_of is None:
             self.made[role].wait_recv()
-
-    def flush(self, *roles):
-        for role in roles:
-            self.made[role].wait_send()
-            self.left.remove(role)
-
-    def drain(self):
-        self.flush(*[role for role in self.made if role in self.left])
+        else:
+            pltpu.make_async_copy(bytes_of, bytes_of, self.rs.at[self.due[role]]).wait()
+
+    def flush(self, out, bytes_of):
+        pltpu.make_async_copy(bytes_of, bytes_of, self.ss.at[self.sent[out]]).wait()
 
 
 def greet(partners):
@@ -57,7 +54,7 @@
     attn, wout_hbm, resid, sin, gain, wg_hbm, wu_hbm, wd_hbm, pj_hbm, tgain, dest,
     out, res, loss,
     w1, xg, wout, part, rp, rq, sp, sq, rp2, rq2, acc, hid, xrow, w2, pj, r1, r2,
-    stat_in, stat_s, loss_in, loss_s, loc, wsem, plane, ss, rs,
+    stat_in, stat_s, loss_in, loss_s, ranks, ta, loc, wsem, plane, ss, rs,
 ):
     x, c, z, y = (lax.axis_index(a) for a in AXES)
     t = z * 4 + y
@@ -100,24 +97,19 @@
     for k in (1, 2, 3):
         pl.semaphore_signal(plane, inc=1, device_id={"y": at(y, k)}, device_id_type=pl.DeviceIdType.MESH)
 
-    def ring_open(tag, axis, base, ref, src=None):
+    def ring_open(out, tag, axis, base, ref, src=None):
         up, down = {axis: at(base, 1)}, {axis: at(base, 3)}
         src = src or (lambda h: ref(0, h))
-        net.send(tag + "LA", src(0), ref(0, 0), up)
-        net.send(tag + "RB", src(1), ref(0, 1), down)
-        net.send(tag + "LB", src(1), ref(0, 1), up)
-        net.send(tag + "RA", src(0), ref(0, 0), down)
-
-    def ring_forward(tag, axis, base, ref):
+        net.send(out, tag + "LA", src(0), ref(0, 0), up)
+        net.send(out, tag + "RB", src(1), ref(0, 1), down)
+        net.send(out, tag + "rest", src(1), ref(0, 1), up)
+        net.send(out, tag + "rest", src(0), ref(0, 0), down)
+
+    def ring_forward(out, tag, axis, base, ref):
         net.got(tag + "LA")
-        net.send(tag + "OA", ref(3, 0), ref(3, 0), {axis: at(base, 1)})
+        net.send(out, tag + "rest", ref(3, 0), ref(3, 0), {axis: at(base, 1)})
         net.got(tag + "RB")
-        net.send(tag + "OB", ref(1, 1), ref(1, 1), {axis: at(base, 3)})
-
-    RING = ("LA", "RB", "LB", "RA", "OA", "OB")
-
-    def ring_close(tag):
-        net.got(*[tag + role for role in RING[2:]])
+        net.send(out, tag + "rest", ref(1, 1), ref(1, 1), {axis: at(base, 3)})
 
     p1 = lambda k, h: xg.at[z, at(y, k), h]
     q1 = lambda k, h: xg.at[at(z, k), y, 2 + h]
@@ -131,32 +123,28 @@
     def shard(role, core):
         return owner[role[0]] * 2 + core, half[role[1]]
 
-    w1_ref = lambda role, core: w1.at[shard(role, core)]
-    w2_ref = lambda role, core: w2.at[shard(role, core)]
-    pj_ref = lambda role, core: pj.at[shard(role, core)]
-
-    def tg_ref(role, core):
-        dd, h = shard(role, core)
-        return w1.at[dd, h, :, pl.ds(0, 512)]
-
-    def along_x_open(tag, ref):
-        for role, own, dev in (("LA", "IA", right), ("RB", "IB", left), ("LB", "IB", right), ("RA", "IA", left)):
-            net.send(tag + role, ref(own, c), ref(own, c), dev)
-        for own in groups[0]:
-            net.send(tag + "s" + own, ref(own, c), ref(own, c), sib)
-
-    def along_x_take(tag, ref, g):
+    def along_x_open(tag, buf):
+        net.send(tag, tag + "LA", buf.at[d, 0], buf.at[d, 0], right)
+        net.send(tag, tag + "RB", buf.at[d, 1], buf.at[d, 1], left)
+        net.send(tag, tag + "near", buf.at[d, 1], buf.at[d, 1], right)
+        net.send(tag, tag + "near", buf.at[d, 0], buf.at[d, 0], left)
+        for h in range(2):
+            net.send(tag, tag + "s0", buf.at[d, h], buf.at[d, h], sib)
+
+    def along_x_take(tag, buf, g):
+        if g == 2:
+            net.got(tag + "near", buf.at[0])
+        if g == 3:
+            net.got(tag + "far", buf.at[0])
         for role in groups[g]:
-            net.got(tag + role)
-            block = ref(role, c)
-            if role == "LA":
-                net.send(tag + "OA", block, block, right)
-            if role == "RB":
-                net.send(tag + "OB", block, block, left)
-            net.send(tag + "s" + role, block, block, sib)
-
-    def sibling_has(tag, g):
-        net.got(*[tag + "s" + role for role in groups[g]])
+            block = buf.at[shard(role, c)]
+            if g == 1:
+                net.got(tag + role)
+                net.send(tag, tag + "far", block, block, right if role == "LA" else left)
+            net.send(tag, f"{tag}s{g}", block, block, sib)
+
+    def sibling_has(tag, buf, g):
+        net.got(f"{tag}s{g}", buf.at[0])
 
     def partial(i):
         b = order[i]
@@ -175,28 +163,27 @@
 
     def sum_send(name, pq, k, j, h, slot, to):
         dev = {"y": at(y, to)} if pq == 0 else {"z": at(z, to)}
-        net.send(f"{name}{pq}{k}", part.at[term(pq, k, j, h)], inbox[pq].at[k, slot], dev)
+        out = "sums" if k else "sums0"
+        net.send(out, f"{name}{pq}{k}", part.at[term(pq, k, j, h)], inbox[pq].at[k, slot], dev)
 
     def sum_open(k):
         for pq in range(2):
             sum_send("fA", pq, k, 2, 0, 0, 1)
             sum_send("fB", pq, k, 2, 1, 1, 3)
-            sum_send("uB", pq, k, 1, 1, 3, 1)
-            sum_send("dA", pq, k, 3, 0, 4, 3)
+            sum_send("u", pq, k, 1, 1, 3, 1)
+            sum_send("u", pq, k, 3, 0, 4, 3)
 
     def sum_pass(k):
         for pq in range(2):
-            for name, j, h, slot, to_slot, send_as, to in (("fA", 1, 0, 0, 2, "uA", 1), ("fB", 3, 1, 1, 5, "dB", 3)):
+            for name, j, h, slot, to_slot, to in (("fA", 1, 0, 0, 2, 1), ("fB", 3, 1, 1, 5, 3)):
                 net.got(f"{name}{pq}{k}")
                 b, rows = term(pq, k, j, h)
                 part[b, rows] = (part[b, rows].astype(F32) + inbox[pq][k, slot].astype(F32)).astype(BF)
-                sum_send(send_as, pq, k, j, h, to_slot, to)
-
-    SUMS = ("fA", "fB", "uB", "dA", "uA", "dB")
+                sum_send("u", pq, k, j, h, to_slot, to)
 
     def sum_close(k):
         for pq in range(2):
-            net.got(*[f"{name}{pq}{k}" for name in ("uA", "uB", "dA", "dB")])
+            net.got(f"u{pq}{k}", inbox[pq].at[k, pl.ds(2, 4)])
             store, box = (sp, rp2) if pq == 0 else (sq, rq2)
             for h in range(2):
                 b, rows = term(pq, k, 0, h)
@@ -208,11 +195,11 @@
                     store[k - 1, h] = s.astype(BF)
             if k:
                 dev = {"z": at(z, k)} if pq == 0 else {"y": at(y, k)}
-                net.send(f"v{pq}{k}", store.at[k - 1], box.at[k - 1], dev)
+                net.send(f"v{pq}", f"v{pq}", store.at[k - 1], box.at[k - 1], dev)
 
     def teacher_hidden():
-        for k in (1, 2, 3):
-            net.got(f"v0{k}", f"v1{k}")
+        net.got("v0", rp2)
+        net.got("v1", rq2)
         for pq, box in ((0, rp2), (1, rq2)):
             rows = slice(pq * 256, pq * 256 + 256)
             s = box[0].astype(F32) + box[1].astype(F32) + box[2].astype(F32)
@@ -249,15 +236,15 @@
         for j in (1, 2, 3):
             if pq == 0:
                 yy = at(y, j)
-                net.send(f"a{g}0{j}", part.at[b, :, yy], r1.at[g, 0, j - 1], {"y": yy})
+                net.send("a", f"a{g}0", part.at[b, :, yy], r1.at[g, 0, j - 1], {"y": yy})
             else:
                 zz = at(z, j)
-                net.send(f"a{g}1{j}", part.at[b, zz], r1.at[g, 1, j - 1], {"z": zz})
+                net.send("a", f"a{g}1", part.at[b, zz], r1.at[g, 1, j - 1], {"z": zz})
 
     own_sum = {}
 
     def middle(g, pq):
-        net.got(*[f"a{g}{pq}{j}" for j in (1, 2, 3)])
+        net.got(f"a{g}{pq}", r1.at[g, pq])
         b = free_blocks[g][pq]
         for k in (1, 2, 3, 0):
             other = at(z if pq == 0 else y, k)
@@ -272,10 +259,10 @@
                 where = (n // 8, n // 4 % 2, n % 4)
                 sp[where] = s.astype(BF)
                 dev = {"z": other} if pq == 0 else {"y": other}
-                net.send(f"b{g}{pq}{k}", sp.at[where], r2.at[g, pq, k - 1], dev)
+                net.send("b", f"b{g}{pq}", sp.at[where], r2.at[g, pq, k - 1], dev)
 
     def finish(g, pq):
-        net.got(*[f"b{g}{pq}{j}" for j in (1, 2, 3)])
+        net.got(f"b{g}{pq}", r2.at[g, pq])
         s = own_sum[g, pq]
         for j in range(3):
             s = s + r2[g, pq, j].astype(F32)
@@ -287,7 +274,7 @@
         ref = xg.at[g, pl.ds(2 * pq, 2), z, y]
         for j in (1, 2, 3):
             dev = {"y": at(y, j)} if pq == 0 else {"z": at(z, j)}
-            net.send(f"c{g}{pq}{j}", ref, ref, dev)
+            net.send("c", f"c{g}{pq}", ref, ref, dev)
 
     def spread_ring(g, pq):
         pair = pl.ds(2 * pq, 2)
@@ -296,15 +283,15 @@
         return f"d{g}1", "y", y, lambda k, h: xg.at[g, pair, pl.ds(2 * h, 2), at(y, k)]
 
     def spread_open(g, pq):
-        net.got(*[f"c{g}{pq}{j}" for j in (1, 2, 3)])
-        ring_open(*spread_ring(g, pq))
+        net.got(f"c{g}{pq}", r2.at[g, pq])
+        ring_open("d", *spread_ring(g, pq))
 
     def spread_forward(g, pq):
-        ring_forward(*spread_ring(g, pq))
+        ring_forward("d", *spread_ring(g, pq))
 
     def predict(g):
-        ring_close(f"d{g}0")
-        ring_close(f"d{g}1")
+        for pq in range(2):
+            net.got(f"d{g}{pq}rest", xg.at[0, 0])
         total = None
         for pq in range(2):
             core = c if pq == 0 else 1 - c
@@ -329,36 +316,74 @@
 
     def stat_open(tag, own, box):
         for n, (i, j) in enumerate(others):
-            net.send(f"{tag}{n}", own, box.at[n], {"z": at(z, i), "y": at(y, j)})
+            net.send(tag, tag, own, box.at[n], {"z": at(z, i), "y": at(y, j)})
 
     def stat_take(tag, own, box):
-        net.got(*[f"{tag}{n}" for n in range(15)])
+        net.got(tag, box)
         total = own[...]
         for n in range(15):
             total = total + box[n]
         return jnp.sum(total, axis=0, keepdims=True)
+
+    def before():
+        first = lax.broadcasted_iota(jnp.int32, (512, 512), 0)
+        later = lax.broadcasted_iota(jnp.int32, (512, 512), 1)
+        return jnp.where(first < later, 1.0, 0.0).astype(BF)
+
+    def dest_of(s):
+        return jnp.concatenate([dest[2 * s], dest[2 * s + 1]], axis=1)
+
+    def unpack_plan():
+        for s in range(8):
+            ranks[s:s + 1, :] = dest_of(s).astype(F32)
+        start = (d * 512).astype(F32)
+        here = ranks[...]
+        here = jnp.where((here >= start) & (here < start + 512.0), 1.0, 0.0)
+        rank = jnp.dot(here.astype(BF), before(), preferred_element_type=F32)
+        ranks[...] = jnp.where(here > 0.0, rank, -1.0)
+        row_id = d * 512 + lax.broadcasted_iota(jnp.int32, (512, 512), 0)
+        slot_id = lax.broadcasted_iota(jnp.int32, (128, 512), 0).astype(F32)
+        for s in range(8):
+            goes = jnp.where(row_id == dest_of(s), 1.0, 0.0).astype(BF)
+            takes = jnp.where(slot_id == ranks[s:s + 1, :], 1.0, 0.0).astype(BF)
+            plan = lax.dot_general(goes, takes, (((1,), (1,)), ((), ())), preferred_element_type=F32)
+            wout[2 + s // 4, :, (s % 4) * 128:(s % 4) * 128 + 128] = plan.astype(BF)
 
     def finish_target():
         scale = lax.rsqrt(stat_take("q", stat_s, stat_in) / HT + 1e-06)
         scale = jnp.broadcast_to(scale, (128, 512)).T
         eight = tgain[pl.ds(pl.multiple_of(lax.div(t, 2) * 8, 8), 8), :].astype(F32)
         four = jnp.where(lax.rem(t, 2) == 0, eight[0:4, :], eight[4:8, :])
-        for h in range(2):
+        for r in range(4):
             for i in range(4):
-                rows, cols = slice(h * 256, h * 256 + 256), slice(i * 128, i * 128 + 128)
-                w1[d, h, :, cols] = (res[rows, cols] * scale[rows, :] * four[i:i + 1, :]).astype(BF)
-
-    row_id = d * 512 + lax.broadcasted_iota(jnp.int32, (512, 256), 0)
-
-    def subtract_target(g):
-        total = None
-        for core in (c, 1 - c):
-            for role in groups[g]:
-                dd, h = shard(role, core)
-                onehot = jnp.where(row_id == dest[dd * 2 + h], 1.0, 0.0).astype(BF)
-                piece = jnp.dot(onehot, w1[dd, h, :, 0:512], preferred_element_type=F32)
-                total = piece if total is None else total + piece
-        res[...] -= total
+                rows, cols = slice(r * 128, r * 128 + 128), slice(i * 128, i * 128 + 128)
+                final = (res[rows, cols] * scale[rows, :] * four[i:i + 1, :]).astype(BF)
+                rp[0, r, :, :, cols] = final.reshape(4, 32, 128)
+        final = rp[0, 0:4].reshape(512, 512)
+        tile = lax.shift_right_logical(dest_of(d), 9)
+        is_tile = jnp.where(lax.broadcasted_iota(jnp.int32, (8, 512), 0) == tile, 1.0, 0.0)
+        rank = jnp.dot(is_tile.astype(BF), before(), preferred_element_type=F32)
+        slot = tile.astype(F32) * 128.0 + jnp.sum(rank * is_tile, axis=0, keepdims=True)
+        slot_id = lax.broadcasted_iota(jnp.int32, (512, 512), 0).astype(F32)
+        for i in range(2):
+            pick = jnp.where(slot_id + 512.0 * i == slot, 1.0, 0.0).astype(BF)
+            wout[i] = jnp.dot(pick, final, preferred_element_type=F32).astype(BF)
+
+    def packed(xx, cc):
+        where = (lax.rem(xx, 2) * 2 + cc) * 128
+        return wout.at[lax.div(xx, 2), pl.ds(pl.multiple_of(where, 128), 128)]
+
+    def target_open():
+        for k, far in ((2, 0), (2, 1), (1, 0), (3, 0), (1, 1), (3, 1), (0, 1)):
+            xx, cc = at(x, k), (1 - c if far else c)
+            net.send("t", "t", packed(xx, cc), ta.at[d], {"x": xx, "c": cc})
+        ta[d] = packed(x, c)[...]
+
+    def subtract_target():
+        net.got("t", ta.at[pl.ds(0, 7)])
+        for i in range(2):
+            rows = ta[4 * i:4 * i + 4].reshape(512, 512)
+            res[...] -= jnp.dot(wout[2 + i], rows, preferred_element_type=F32)
 
     def both(step, g):
         step(g, 0)
@@ -366,49 +391,50 @@
 
     def downs(g):
         down(g, 0)
-        sibling_has("m", g)
+        sibling_has("m", w2, g)
         down(g, 1)
 
-    ring_open("p1", "y", y, p1, lambda h: sin.at[h])
-    ring_open("q1", "z", z, q1, lambda h: sin.at[2 + h])
+    ring_open("near", "p1", "y", y, p1, lambda h: sin.at[h])
+    ring_open("near", "q1", "z", z, q1, lambda h: sin.at[2 + h])
     for cp in loads[:4]:
         cp.wait()
-    along_x_open("w", w1_ref)
+    along_x_open("w", w1)
     for i in range(SLOTS):
         wloads[i].start()
     for cp in w2_loads + pj_loads:
         cp.start()
     for i in range(5):
         partial(i)
-    ring_forward("p1", "y", y, p1)
-    ring_forward("q1", "z", z, q1)
+    ring_forward("near", "p1", "y", y, p1)
+    ring_forward("near", "q1", "z", z, q1)
     sum_open(1)
     partial(5)
     partial(6)
     loads[4].wait()
-    ring_close("p1")
-    ring_open("p2", "z", z, p2)
-    ring_close("q1")
-    ring_open("q2", "y", y, q2)
+    net.got("p1rest", xg.at[0, 0])
+    ring_open("wide", "p2", "z", z, p2)
+    net.got("q1rest", xg.at[0, 0])
+    ring_open("wide", "q2", "y", y, q2)
     partial(7)
     partial(8)
     sum_pass(1)
     for i in range(9, 16):
         partial(i)
     sum_open(2)
-    ring_forward("p2", "z", z, p2)
-    ring_forward("q2", "y", y, q2)
+    ring_forward("wide", "p2", "z", z, p2)
+    ring_forward("wide", "q2", "y", y, q2)
     sum_open(3)
-    along_x_take("w", w1_ref, 1)
+    along_x_take("w", w1, 1)
     for cp in w2_loads:
         cp.wait()
-    along_x_open("m", w2_ref)
+    along_x_open("m", w2)
     sum_pass(2)
     sum_open(0)
-    ring_close("p2")
-    ring_close("q2")
-    for tag in ("p1", "q1", "p2", "q2"):
-        net.flush(*[tag + role for role in RING])
+    unpack_plan()
+    net.got("p2rest", xg.at[0])
+    net.got("q2rest", xg.at[0])
+    net.flush("near", xg.at[0, pl.ds(0, 3)])
+    net.flush("wide", xg.at[pl.ds(0, 3)])
     xrow[...] = xg[:, :, z, y].reshape(16, 32, 256)
 
     @pl.loop(0, 4)
@@ -424,19 +450,19 @@
             xg[s // 4, s % 4, r] = (v * scale * g.astype(F32)).astype(BF).reshape(4, 32, 256)
 
     sum_pass(3)
-    sibling_has("w", 0)
+    sibling_has("w", w1, 0)
     gate_up(0)
     sum_close(1)
-    sibling_has("w", 1)
+    sibling_has("w", w1, 1)
     gate_up(1)
-    along_x_take("w", w1_ref, 2)
+    along_x_take("w", w1, 2)
     sum_pass(0)
     sum_close(2)
-    sibling_has("w", 2)
+    sibling_has("w", w1, 2)
     gate_up(2)
     sum_close(3)
-    along_x_take("w", w1_ref, 3)
-    sibling_has("w", 3)
+    along_x_take("w", w1, 3)
+    sibling_has("w", w1, 3)
     gate_up(3)
 
     @pl.loop(0, 7)
@@ -445,15 +471,14 @@
         u = acc[:, pl.ds(pl.multiple_of(896 + j * 128, 128), 128)]
         hid[:, pl.ds(pl.multiple_of(j * 128, 128), 128)] = (jax.nn.silu(g) * u).astype(BF)
 
-    net.flush(*[f"{name}{pq}{k}" for name in SUMS for pq in range(2) for k in (1, 2, 3)])
-    net.flush(*[f"v0{k}" for k in (1, 2, 3)])
+    net.flush("sums", part.at[pl.ds(0, 9)])
+    net.flush("v0", sp)
     downs(0)
-    net.flush(*["w" + s + role for g in groups for role in g for s in ("", "s") if s or role[0] != "I"])
     for cp in pj_loads:
         cp.wait()
     sum_close(0)
-    along_x_take("m", w2_ref, 1)
-    along_x_open("p", pj_ref)
+    along_x_take("m", w2, 1)
+    along_x_open("p", pj)
     downs(1)
     both(middle, 0)
     teacher_hidden()
@@ -462,39 +487,36 @@
     stat_open("q", stat_s, stat_in)
     both(middle, 1)
     both(finish, 0)
-    along_x_take("m", w2_ref, 2)
+    along_x_take("m", w2, 2)
     downs(2)
     both(finish, 1)
     both(spread_open, 0)
     finish_target()
+    target_open()
     both(middle, 2)
-    along_x_take("m", w2_ref, 3)
+    along_x_take("m", w2, 3)
     downs(3)
     both(spread_open, 1)
     both(spread_forward, 0)
     both(finish, 2)
-    along_x_take("p", pj_ref, 1)
-    sibling_has("p", 0)
-    along_x_open("t", tg_ref)
+    along_x_take("p", pj, 1)
     both(middle, 3)
-    along_x_take("p", pj_ref, 2)
+    along_x_take("p", pj, 2)
     both(spread_forward, 1)
     both(spread_open, 2)
+    sibling_has("p", pj, 0)
     predict(0)
     both(finish, 3)
-    along_x_take("p", pj_ref, 3)
+    along_x_take("p", pj, 3)
     both(spread_forward, 2)
-    sibling_has("p", 1)
+    sibling_has("p", pj, 1)
     predict(1)
     both(spread_open, 3)
-    along_x_take("t", tg_ref, 1)
     both(spread_forward, 3)
-    sibling_has("p", 2)
+    sibling_has("p", pj, 2)
     predict(2)
-    sibling_has("t", 0)
-    subtract_target(0)
-    along_x_take("t", tg_ref, 2)
-    sibling_has("p", 3)
+    subtract_target()
+    sibling_has("p", pj, 3)
     predict(3)
 
     h0 = lax.rem(t, 2)
@@ -505,17 +527,15 @@
     i0 = (1 - k_odd) * h0 + k_odd * (1 - k_two)
     out[...] = xg[g0, 2 * lax.rem(d0 + c, 2) + i0].reshape(512, 256)
 
-    sibling_has("t", 1)
-    subtract_target(1)
-    sibling_has("t", 2)
-    subtract_target(2)
-    along_x_take("t", tg_ref, 3)
-    sibling_has("t", 3)
-    subtract_target(3)
     loss_s[...] = row_squares(res[...])
     stat_open("l", loss_s, loss_in)
     loss[...] = stat_take("l", loss_s, loss_in) / HT
-    net.drain()
+    for out_tag, ref in (
+        ("w", w1.at[pl.ds(0, 7)]), ("m", w2.at[pl.ds(0, 7)]), ("p", pj.at[pl.ds(0, 7)]),
+        ("t", ta.at[pl.ds(0, 7)]), ("sums0", part.at[pl.ds(0, 3)]), ("v1", sq), ("a", part.at[pl.ds(0, 6)]),
+        ("b", r2), ("c", r2), ("d", xg.at[pl.ds(0, 3)]), ("q", stat_in), ("l", loss_in),
+    ):
+        net.flush(out_tag, ref)
 
 
 def call_kernel(*args):
@@ -553,11 +573,13 @@
             pltpu.VMEM((8, 512), F32),
             pltpu.VMEM((15, 8, 512), F32),
             pltpu.VMEM((8, 512), F32),
+            pltpu.VMEM((8, 512), F32),
+            pltpu.VMEM((8, 128, 512), BF),
             pltpu.SemaphoreType.DMA((9,)),
             pltpu.SemaphoreType.DMA((4,)),
             pltpu.SemaphoreType.REGULAR,
-            pltpu.SemaphoreType.DMA((TRANSFERS,)),
-            pltpu.SemaphoreType.DMA((TRANSFERS,)),
+            pltpu.SemaphoreType.DMA((SENDS,)),
+            pltpu.SemaphoreType.DMA((RECEIVES,)),
         ],
         compiler_params=pltpu.CompilerParams(
             collective_id=0, has_side_effects=True, vmem_limit_bytes=67043328

time: 158 us -> 150 us (0.949)
  Pallas kernels: 157 us -> 149 us
    pallas_call x1, Pallas kernels: 154 us -> 147 us  [call_kernel(): pl.pallas_call(kernel, name='first', out_shape=(jax.ShapeDtypeStruct((512...]
where the time goes in v5:
time: 150 us
  Pallas kernels  149 us (99%)
    pallas_call x1, Pallas kernels, call_kernel(): pl.pallas_call(kernel, name='first', out_shape=(jax.ShapeDtypeStruct((512...  147 us

profile of v5, /device:TPU:0, one launch (start us, length us, event | category | flops | bytes accessed | tf_op | source)
XLA Modules:
  0.0 149.6 jit_solution(13697685698364942624)
XLA Ops:
  0.6 146.5 %first.1 = (bf16[512,256]{1,0:T(8,128)(2,1)}, f32[512,512]{1,0:T(8,128)}, f32[1,512]{1,0:T(1,128)}) custom-call(bf16[512,512]{1,0:T(8,128)(2,1)} %attn.1, bf16[512,8192]{1,0:T(8,128)(2,1)} %wout_hbm.1, bf16[32,8192]{1,0:T(8,128)(2,1)} %resid.1, bf16[4,4,32,256]{3,2,1,0:T(8,128)(2,1)} %bitcast.5, bf16[32,128]{1,0:T(8,128)(2,1)} %bitcast.8, ...), custom_call_target="tpu_custom_call" | custom-call | tf_op jit(solution)/shard_map/first/pallas_call | solution.py:544
  147.2 2.4 %keep.1 = (bf16[512,256]{1,0:T(8,128)(2,1)}, f32[512,512]{1,0:T(8,128)}, f32[1,512]{1,0:T(1,128)}) custom-call(bf16[512,256]{1,0:T(8,128)(2,1)} %get-tuple-element.9.out, f32[512,512]{1,0:T(8,128)} %get-tuple-element.10.res, f32[1,512]{1,0:T(1,128)} %get-tuple-element.11.loss), custom_call_target="tpu_custom_call" | custom-call | tf_op jit(solution)/shard_map/keep/pallas_call | solution.py:623

commit v6 on v5

--- a/solution.py
+++ b/solution.py
@@ -12,7 +12,7 @@
 AXES = ("x", "c", "z", "y")
 TENSOR = ("z", "y")
 DP = ("x", "c")
-SENDS, RECEIVES = 16, 113
+SENDS, RECEIVES = 16, 129
 
 
 class Net:
@@ -52,8 +52,8 @@
 
 def kernel(
     attn, wout_hbm, resid, sin, gain, wg_hbm, wu_hbm, wd_hbm, pj_hbm, tgain, dest,
-    out, res, loss,
-    w1, xg, wout, part, rp, rq, sp, sq, rp2, rq2, acc, hid, xrow, w2, pj, r1, r2,
+    out, res_out, loss,
+    res, w1, xg, wout, part, rp, rq, sp, sq, rp2, rq2, acc, hid, xrow, w2, pj, r1, r2,
     stat_in, stat_s, loss_in, loss_s, ranks, ta, loc, wsem, plane, ss, rs,
 ):
     x, c, z, y = (lax.axis_index(a) for a in AXES)
@@ -130,6 +130,42 @@
         net.send(tag, tag + "near", buf.at[d, 0], buf.at[d, 0], left)
         for h in range(2):
             net.send(tag, tag + "s0", buf.at[d, h], buf.at[d, h], sib)
+
+    quarters = (pl.ds(0, 128), pl.ds(128, 128))
+
+    def w1_forward():
+        for i, rows in enumerate(quarters):
+            for role, dev in (("LA", right), ("RB", left)):
+                if i == 0:
+                    net.got("w" + role)
+                block = w1.at[shard(role, c) + (rows,)]
+                net.send("w", f"wfar{i}", block, block, dev)
+        for role in groups[1]:
+            block = w1.at[shard(role, c)]
+            net.send("w", "ws1", block, block, sib)
+
+    def w2_forward():
+        for u, cols in enumerate(quarters):
+            for role, dev in (("LA", right), ("RB", left)):
+                if u == 0:
+                    net.got("m" + role)
+                block = w2.at[shard(role, c) + (slice(None), cols)]
+                net.send("m", f"mfar{u}", block, block, dev)
+        for role in groups[1]:
+            block = w2.at[shard(role, c)]
+            net.send("m", "ms1", block, block, sib)
+
+    def w2_far(u):
+        net.got(f"mfar{u}", w2.at[0, 0])
+        for role in groups[3]:
+            block = w2.at[shard(role, c) + (slice(None), quarters[u])]
+            net.send("m", f"ms3{u}", block, block, sib)
+
+    def w1_far(i):
+        net.got(f"wfar{i}", w1.at[0, 0])
+        for role in groups[3]:
+            block = w1.at[shard(role, c) + (quarters[i],)]
+            net.send("w", f"ws3{i}", block, block, sib)
 
     def along_x_take(tag, buf, g):
         if g == 2:
@@ -208,99 +244,125 @@
     def slot_of(role, core):
         return xg.at[owner[role[0]], 2 * core + half[role[1]]]
 
-    def gate_up(g):
+    def gate_up(g, i=None):
         @pl.loop(0, 7)
         def _(j):
             cols = pl.ds(pl.multiple_of(j * 256, 256), 256)
             total = None
             for core in (c, 1 - c):
-                for role in groups[g]:
-                    dd, h = shard(role, core)
-                    lhs = slot_of(role, core)[...].reshape(512, 256)
-                    term = jnp.dot(lhs, w1[dd, h, :, cols], preferred_element_type=F32)
-                    total = term if total is None else total + term
+                both_roles = [(slot_of(role, core), w1.at[shard(role, core)]) for role in groups[g]]
+                if i is None:
+                    pairs = [(lhs[...].reshape(512, 256), rhs[:, cols]) for lhs, rhs in both_roles]
+                else:
+                    part_of = slice(i * 128, i * 128 + 128)
+                    lhs = [lhs[..., part_of].reshape(512, 128) for lhs, rhs in both_roles]
+                    rhs = [rhs[part_of, cols] for lhs_, rhs in both_roles]
+                    pairs = [(jnp.concatenate(lhs, axis=1), jnp.concatenate(rhs, axis=0))]
+                for lhs, rhs in pairs:
+                    piece = jnp.dot(lhs, rhs, preferred_element_type=F32)
+                    total = piece if total is None else total + piece
             if g == 0:
                 acc[:, cols] = total
             else:
                 acc[:, cols] += total
 
+    steps = ((0, (0, 1)), (1, (0, 1)), (2, (0, 1)), (3, (0,)), (3, (1,)))
     free_blocks = ((5, 6), (7, 9), (10, 11), (13, 14))
 
-    def down(g, pq):
-        core = c if pq == 0 else 1 - c
+    def pieces(g, pq):
+        return [shard(role, c if pq == 0 else 1 - c) for role in groups[g]]
+
+    def lanes_of(n):
+        us = steps[n][1]
+        return pl.ds(us[0] * 256, len(us) * 256)
+
+    def down(n, pq):
+        g, us = steps[n]
         b = free_blocks[g][pq]
-        for i in range(2):
-            dd, h = shard(groups[g][i], core)
-            piece = jnp.dot(hid[...], w2[dd, h], preferred_element_type=F32)
-            part[b, :, :, :, i * 256:(i + 1) * 256] = piece.astype(BF).reshape(4, 4, 32, 256)
+        lanes = lanes_of(n)
+        for u in us:
+            cut = slice(u * 128, u * 128 + 128)
+            rhs = jnp.concatenate([w2[dd, h, :, cut] for dd, h in pieces(g, pq)], axis=1)
+            piece = jnp.dot(hid[...], rhs, preferred_element_type=F32)
+            part[b, :, :, :, u * 256:(u + 1) * 256] = piece.astype(BF).reshape(4, 4, 32, 256)
         for j in (1, 2, 3):
+            to = r1.at[g, pq, j - 1, :, :, lanes]
             if pq == 0:
                 yy = at(y, j)
-                net.send("a", f"a{g}0", part.at[b, :, yy], r1.at[g, 0, j - 1], {"y": yy})
+                net.send("a", f"a{n}0", part.at[b, :, yy, :, lanes], to, {"y": yy})
             else:
                 zz = at(z, j)
-                net.send("a", f"a{g}1", part.at[b, zz], r1.at[g, 1, j - 1], {"z": zz})
+                net.send("a", f"a{n}1", part.at[b, zz, :, :, lanes], to, {"z": zz})
 
     own_sum = {}
 
-    def middle(g, pq):
-        net.got(f"a{g}{pq}", r1.at[g, pq])
+    def middle(n, pq):
+        g, us = steps[n]
+        lanes = lanes_of(n)
+        net.got(f"a{n}{pq}", r1.at[g, pq, :, :, :, lanes])
         b = free_blocks[g][pq]
         for k in (1, 2, 3, 0):
             other = at(z if pq == 0 else y, k)
-            mine = part[b, other, y] if pq == 0 else part[b, z, other]
+            mine = part[b, other, y, :, lanes] if pq == 0 else part[b, z, other, :, lanes]
             s = mine.astype(F32)
             for j in range(3):
-                s = s + r1[g, pq, j, other].astype(F32)
+                s = s + r1[g, pq, j, other, :, lanes].astype(F32)
             if k == 0:
-                own_sum[g, pq] = s
+                own_sum[n, pq] = s
             else:
-                n = (2 * g + pq) * 3 + k - 1
-                where = (n // 8, n // 4 % 2, n % 4)
+                i = (2 * g + pq) * 3 + k - 1
+                where = (i // 8, i // 4 % 2, i % 4, slice(None), lanes)
                 sp[where] = s.astype(BF)
                 dev = {"z": other} if pq == 0 else {"y": other}
-                net.send("b", f"b{g}{pq}", sp.at[where], r2.at[g, pq, k - 1], dev)
-
-    def finish(g, pq):
-        net.got(f"b{g}{pq}", r2.at[g, pq])
-        s = own_sum[g, pq]
+                net.send("b", f"b{n}{pq}", sp.at[where], r2.at[g, pq, k - 1, :, lanes], dev)
+
+    def finish(n, pq):
+        g, us = steps[n]
+        lanes = lanes_of(n)
+        net.got(f"b{n}{pq}", r2.at[g, pq, :, :, lanes])
+        s = own_sum[n, pq]
         for j in range(3):
-            s = s + r2[g, pq, j].astype(F32)
-        core = c if pq == 0 else 1 - c
-        for i in range(2):
-            dd, h = shard(groups[g][i], core)
-            xin = xrow[dd * 2 + h].astype(F32)
-            xg[g, 2 * pq + i, z, y] = (xin + s[:, i * 256:(i + 1) * 256]).astype(BF)
-        ref = xg.at[g, pl.ds(2 * pq, 2), z, y]
+            s = s + r2[g, pq, j, :, lanes].astype(F32)
+        for i, u in enumerate(us):
+            cut = slice(u * 128, u * 128 + 128)
+            xin = jnp.concatenate([xrow[dd * 2 + h, :, cut] for dd, h in pieces(g, pq)], axis=1)
+            mlp = s[:, i * 256:(i + 1) * 256]
+            xg[g, 2 * pq + u, z, y] = (xin.astype(F32) + mlp).astype(BF)
+        ref = xg.at[g, pl.ds(2 * pq + us[0], len(us)), z, y]
         for j in (1, 2, 3):
             dev = {"y": at(y, j)} if pq == 0 else {"z": at(z, j)}
-            net.send("c", f"c{g}{pq}", ref, ref, dev)
-
-    def spread_ring(g, pq):
-        pair = pl.ds(2 * pq, 2)
+            net.send("c", f"c{n}{pq}", ref, ref, dev)
+
+    def spread_ring(n, pq):
+        g, us = steps[n]
+        pair = pl.ds(2 * pq + us[0], len(us))
         if pq == 0:
-            return f"d{g}0", "z", z, lambda k, h: xg.at[g, pair, at(z, k), pl.ds(2 * h, 2)]
-        return f"d{g}1", "y", y, lambda k, h: xg.at[g, pair, pl.ds(2 * h, 2), at(y, k)]
-
-    def spread_open(g, pq):
-        net.got(f"c{g}{pq}", r2.at[g, pq])
-        ring_open("d", *spread_ring(g, pq))
-
-    def spread_forward(g, pq):
-        ring_forward("d", *spread_ring(g, pq))
-
-    def predict(g):
+            return f"d{n}0", "z", z, lambda k, h: xg.at[g, pair, at(z, k), pl.ds(2 * h, 2)]
+        return f"d{n}1", "y", y, lambda k, h: xg.at[g, pair, pl.ds(2 * h, 2), at(y, k)]
+
+    def spread_open(n, pq):
+        g, us = steps[n]
+        net.got(f"c{n}{pq}", r2.at[g, pq, :, :, lanes_of(n)])
+        ring_open("d", *spread_ring(n, pq))
+
+    def spread_forward(n, pq):
+        ring_forward("d", *spread_ring(n, pq))
+
+    def spread_close(n):
         for pq in range(2):
-            net.got(f"d{g}{pq}rest", xg.at[0, 0])
+            net.got(f"d{n}{pq}rest", xg.at[0, 0, pl.ds(0, 2 * len(steps[n][1]))])
+
+    def predict(n, first=False):
+        g, us = steps[n]
         total = None
         for pq in range(2):
-            core = c if pq == 0 else 1 - c
-            for i in range(2):
-                dd, h = shard(groups[g][i], core)
-                lhs = xg[g, 2 * pq + i].reshape(512, 256)
-                piece = jnp.dot(lhs, pj[dd, h], preferred_element_type=F32)
+            for u in us:
+                cut = slice(u * 128, u * 128 + 128)
+                rhs = jnp.concatenate([pj[dd, h, cut, :] for dd, h in pieces(g, pq)], axis=0)
+                lhs = xg[g, 2 * pq + u].reshape(512, 256)
+                piece = jnp.dot(lhs, rhs, preferred_element_type=F32)
                 total = piece if total is None else total + piece
-        if g == 0:
+        if first:
             res[...] = total
         else:
             res[...] += total
@@ -389,10 +451,13 @@
         step(g, 0)
         step(g, 1)
 
-    def downs(g):
-        down(g, 0)
-        sibling_has("m", w2, g)
-        down(g, 1)
+    def downs(n):
+        down(n, 0)
+        if n < 3:
+            sibling_has("m", w2, n)
+        else:
+            net.got(f"ms3{n - 3}", w2.at[0, 0])
+        down(n, 1)
 
     ring_open("near", "p1", "y", y, p1, lambda h: sin.at[h])
     ring_open("near", "q1", "z", z, q1, lambda h: sin.at[2 + h])
@@ -424,7 +489,7 @@
     ring_forward("wide", "p2", "z", z, p2)
     ring_forward("wide", "q2", "y", y, q2)
     sum_open(3)
-    along_x_take("w", w1, 1)
+    w1_forward()
     for cp in w2_loads:
         cp.wait()
     along_x_open("m", w2)
@@ -461,9 +526,10 @@
     sibling_has("w", w1, 2)
     gate_up(2)
     sum_close(3)
-    along_x_take("w", w1, 3)
-    sibling_has("w", w1, 3)
-    gate_up(3)
+    for i in range(2):
+        w1_far(i)
+        net.got(f"ws3{i}", w1.at[0, 0])
+        gate_up(3, i)
 
     @pl.loop(0, 7)
     def _(j):
@@ -473,50 +539,90 @@
 
     net.flush("sums", part.at[pl.ds(0, 9)])
     net.flush("v0", sp)
-    downs(0)
-    for cp in pj_loads:
-        cp.wait()
+    sibling_has("m", w2, 0)
+    down(0, 1)
+    down(0, 0)
+    w2_forward()
+    sibling_has("m", w2, 1)
+    down(1, 1)
     sum_close(0)
-    along_x_take("m", w2, 1)
-    along_x_open("p", pj)
-    downs(1)
-    both(middle, 0)
     teacher_hidden()
     stat_s[...] = row_squares(res[...])
     pl.semaphore_wait(plane, 3)
     stat_open("q", stat_s, stat_in)
-    both(middle, 1)
-    both(finish, 0)
+    down(1, 0)
     along_x_take("m", w2, 2)
-    downs(2)
-    both(finish, 1)
-    both(spread_open, 0)
+    middle(0, 1)
+    down(2, 0)
+    middle(0, 0)
+    sibling_has("m", w2, 2)
+    down(2, 1)
+    for cp in pj_loads:
+        cp.wait()
+    along_x_open("p", pj)
+    finish(0, 0)
+    finish(0, 1)
+    w2_far(0)
+    middle(1, 1)
     finish_target()
     target_open()
-    both(middle, 2)
-    along_x_take("m", w2, 3)
-    downs(3)
-    both(spread_open, 1)
-    both(spread_forward, 0)
-    both(finish, 2)
+    net.got("ms30", w2.at[0, 0])
+    down(3, 1)
+    w2_far(1)
+    middle(1, 0)
+    down(3, 0)
+    middle(2, 1)
+    net.got("ms31", w2.at[0, 0])
+    down(4, 1)
+    down(4, 0)
+    spread_open(0, 1)
+    finish(1, 1)
+    middle(3, 1)
+    middle(2, 0)
+    middle(3, 0)
+    finish(1, 0)
+    spread_open(0, 0)
+    finish(2, 1)
+    middle(4, 1)
+    spread_forward(0, 1)
+    middle(4, 0)
+    finish(2, 0)
+    finish(3, 0)
     along_x_take("p", pj, 1)
-    both(middle, 3)
+    spread_forward(0, 0)
+    finish(3, 1)
+    spread_open(1, 0)
+    spread_open(1, 1)
+    finish(4, 0)
+    finish(4, 1)
+    sibling_has("p", pj, 0)
+    spread_close(0)
+    predict(0, True)
+    spread_open(2, 1)
+    spread_open(2, 0)
+    subtract_target()
     along_x_take("p", pj, 2)
-    both(spread_forward, 1)
-    both(spread_open, 2)
-    sibling_has("p", pj, 0)
-    predict(0)
-    both(finish, 3)
+    spread_open(3, 0)
+    spread_open(3, 1)
+    spread_open(4, 0)
+    spread_open(4, 1)
+    spread_forward(2, 1)
+    spread_forward(2, 0)
+    spread_forward(1, 0)
+    spread_forward(1, 1)
+    spread_forward(3, 1)
+    spread_forward(3, 0)
+    spread_forward(4, 1)
     along_x_take("p", pj, 3)
-    both(spread_forward, 2)
+    spread_forward(4, 0)
+    sibling_has("p", pj, 2)
+    spread_close(2)
+    predict(2)
     sibling_has("p", pj, 1)
+    spread_close(1)
     predict(1)
-    both(spread_open, 3)
-    both(spread_forward, 3)
-    sibling_has("p", pj, 2)
-    predict(2)
-    subtract_target()
     sibling_has("p", pj, 3)
+    spread_close(3)
     predict(3)
 
     h0 = lax.rem(t, 2)
@@ -525,11 +631,27 @@
     k_odd, k_two = lax.rem(k0, 2), lax.div(k0, 2)
     g0 = (1 - k_odd) * k_two * 3 + k_odd * (k_two * (1 + h0) + (1 - k_two) * (2 - h0))
     i0 = (1 - k_odd) * h0 + k_odd * (1 - k_two)
-    out[...] = xg[g0, 2 * lax.rem(d0 + c, 2) + i0].reshape(512, 256)
-
+    own_lanes = pl.ds(pl.multiple_of(i0 * 128, 128), 128)
+    put_out = [
+        pltpu.make_async_copy(
+            xg.at[g0, 2 * lax.rem(d0 + c, 2) + u, :, :, :, own_lanes],
+            out.at[:, :, :, pl.ds(u * 128, 128)],
+            loc.at[u],
+        )
+        for u in range(2)
+    ]
+    put_res = pltpu.make_async_copy(res, res_out, loc.at[2])
+    spread_close(4)
+    for cp in put_out:
+        cp.start()
+    predict(4)
+    put_res.start()
     loss_s[...] = row_squares(res[...])
     stat_open("l", loss_s, loss_in)
     loss[...] = stat_take("l", loss_s, loss_in) / HT
+    for cp in put_out:
+        cp.wait()
+    put_res.wait()
     for out_tag, ref in (
         ("w", w1.at[pl.ds(0, 7)]), ("m", w2.at[pl.ds(0, 7)]), ("p", pj.at[pl.ds(0, 7)]),
         ("t", ta.at[pl.ds(0, 7)]), ("sums0", part.at[pl.ds(0, 3)]), ("v1", sq), ("a", part.at[pl.ds(0, 6)]),
@@ -545,13 +667,14 @@
         kernel,
         name="first",
         out_shape=(
-            jax.ShapeDtypeStruct((512, 256), BF),
+            jax.ShapeDtypeStruct((4, 4, 32, 256), BF),
             jax.ShapeDtypeStruct((512, 512), F32),
             jax.ShapeDtypeStruct((1, 512), F32),
         ),
         in_specs=[vm, hb, vm, vm, vm, hb, hb, hb, hb, vm, vm],
-        out_specs=(vm, vm, vm),
+        out_specs=(hb, hb, vm),
         scratch_shapes=[
+            pltpu.VMEM((512, 512), F32),
             pltpu.VMEM((8, 2, 256, 1792), BF),
             pltpu.VMEM((4, 4, 4, 4, 32, 256), BF),
             pltpu.VMEM((4, 512, 512), BF),
@@ -587,10 +710,21 @@
     )(*args)
 
 
-def keep(out, res, loss, out_to, res_to, loss_to):
-    out_to[...] = out[...]
-    res_to[...] = res[...]
-    loss_to[...] = loss[...]
+def keep(*refs):
+    sources, results, held, sems = refs[0:3], refs[3:6], refs[6:9], refs[9]
+    pieces = []
+    for n, (a, v, o) in enumerate(zip(sources, held, results)):
+        cuts = [slice(None)] if n else [pl.ds(i, 1) for i in range(4)]
+        pieces += [(a.at[cut], v.at[cut], o.at[cut]) for cut in cuts]
+    inward = [pltpu.make_async_copy(a, v, sems.at[i]) for i, (a, v, o) in enumerate(pieces)]
+    outward = [pltpu.make_async_copy(v, o, sems.at[i]) for i, (a, v, o) in enumerate(pieces)]
+    for cp in inward:
+        cp.start()
+    for before, after in zip(inward, outward):
+        before.wait()
+        after.start()
+    for cp in outward:
+        cp.wait()
 
 
 def local(
@@ -606,7 +740,7 @@
     w_down,
     proj,
 ):
-    made = call_kernel(
+    out, residue, loss = call_kernel(
         attn_ctx,
         w_out,
         resid,
@@ -619,15 +753,17 @@
         teacher_gain.reshape(64, 128),
         dest_row.reshape(16, 1, 256),
     )
-    vm = pl.BlockSpec(memory_space=pltpu.VMEM)
-    out, residue, loss = pl.pallas_call(
+    made = (residue.reshape(4, 128, 512), out.reshape(512, 256), loss)
+    hb = pl.BlockSpec(memory_space=pl.ANY)
+    residue, out, loss = pl.pallas_call(
         keep,
         name="keep",
         out_shape=tuple(jax.ShapeDtypeStruct(a.shape, a.dtype) for a in made),
-        in_specs=[vm, vm, vm],
-        out_specs=(vm, vm, vm),
+        in_specs=[hb, hb, hb],
+        out_specs=(hb, hb, hb),
+        scratch_shapes=[pltpu.VMEM(a.shape, a.dtype) for a in made] + [pltpu.SemaphoreType.DMA((6,))],
     )(*made)
-    return (out, loss.reshape(512), residue)
+    return (out, loss.reshape(512), residue.reshape(512, 512))
 
 
 def solution(mesh):

time: 150 us -> 145 us (0.967)
  Pallas kernels: 149 us -> 144 us
    pallas_call x1, Pallas kernels: 147 us -> 142 us  [call_kernel(): pl.pallas_call(kernel, name='first', out_shape=(jax.ShapeDtypeStruct((4,...]
where the time goes in v6:
time: 145 us
  Pallas kernels  144 us (99%)
    pallas_call x1, Pallas kernels, call_kernel(): pl.pallas_call(kernel, name='first', out_shape=(jax.ShapeDtypeStruct((4,...  142 us

profile of v6, /device:TPU:0, one launch (start us, length us, event | category | flops | bytes accessed | tf_op | source)
XLA Modules:
  0.0 144.5 jit_solution(10491758452625009582)
XLA Ops:
  0.6 141.7 %first.1 = (bf16[4,4,32,256]{3,2,1,0:T(8,128)(2,1)}, f32[512,512]{1,0:T(8,128)}, f32[1,512]{1,0:T(1,128)}) custom-call(bf16[512,512]{1,0:T(8,128)(2,1)} %attn.1, bf16[512,8192]{1,0:T(8,128)(2,1)} %wout_hbm.1, bf16[32,8192]{1,0:T(8,128)(2,1)} %resid.1, bf16[4,4,32,256]{3,2,1,0:T(8,128)(2,1)} %bitcast.9, bf16[32,128]{1,0:T(8,128)(2,1)} %bitcast.13, ...), custom_call_target="tpu_custom_call" | custom-call | tf_op jit(solution)/shard_map/first/pallas_call | solution.py:666
  142.3 2.1 %keep.1 = (f32[4,128,512]{2,1,0:T(8,128)}, bf16[512,256]{1,0:T(8,128)(2,1)}, f32[1,512]{1,0:T(1,128)}) custom-call(f32[4,128,512]{2,1,0:T(8,128)} %bitcast.8, bf16[512,256]{1,0:T(8,128)(2,1)} %bitcast.10, f32[1,512]{1,0:T(1,128)} %get-tuple-element.11.refs_2_), custom_call_target="tpu_custom_call" | custom-call | tf_op jit(solution)/shard_map/keep/pallas_call | solution.py:758
